TPU v7x, 256 devices: a whole 4x4x8 slice. The times are simulated.
256 devices in a mesh: member: 2 (over y_lo), lat: 8 (over x, core), lon: 16 (over z, y_hi).
Axes of the slice: x: 4, y: 4 (y_hi: 2, y_lo: 2; y = y_hi * 2 + y_lo), z: 8, core: 2. Of those that a mesh axis runs over, the one named last changes fastest.
Arguments:
- fields: float32 [4, 192, 64, 2048], P('member', None, 'lat', 'lon'), parts along dimension 0, may hold values from -6 to 6
- wind_east: float32 [64, 2048], P('lat', 'lon'), may hold values from -0.3 to 0.3
- wind_north: float32 [64, 2048], P('lat', 'lon'), may hold values from -0.3 to 0.3
- diffusion: float32 [64, 2048], P('lat', 'lon'), may hold values from 0.01 to 0.08
- inflow_owner: int32 [2048, 1], P(('lat', 'lon')), may hold values from 0 to 15; in each aligned block of 16 rows (0 to 15, 16 to 31, ...) at most 2 rows name the same one
- inflow_cell: int32 [2048, 128], P(('lat', 'lon')), may hold values from 0 to 1023
- inflow_node: int32 [2048, 128], P(('lat', 'lon')), may hold values from 0 to 255
- inflow_weight: float32 [2048, 128], P(('lat', 'lon')), may hold values from 0.25 to 1.5
- encoder: bfloat16 [192, 512], replicated, may hold values from -0.21875 to 0.21875
- sender_weight: bfloat16 [2, 512, 512], replicated, may hold values from -0.25 to 0.25
- receiver_weight: bfloat16 [2, 512, 512], replicated, may hold values from -0.25 to 0.25
- update_weight: bfloat16 [2, 512, 512], replicated, may hold values from -0.25 to 0.25
- decoder: bfloat16 [512, 192], replicated, may hold values from -0.25 to 0.25
- edge_sender: int32 [8, 16, 1536], P('lat', 'lon'), may hold values from 0 to 447, as said below
- edge_receiver: int32 [8, 16, 1536], P('lat', 'lon'), may hold values from 0 to 255
- halo_rows: int32 [8, 16, 4, 48], P('lat', 'lon'), may hold values from 0 to 255
- outflow_owner: int32 [2048, 1], P(('lat', 'lon')), may hold values from 0 to 15; in each aligned block of 16 rows (0 to 15, 16 to 31, ...) at most 2 rows name the same one
- outflow_node: int32 [2048, 128], P(('lat', 'lon')), may hold values from 0 to 255
- outflow_cell: int32 [2048, 128], P(('lat', 'lon')), may hold values from 0 to 1023
- outflow_weight: float32 [2048, 128], P(('lat', 'lon')), may hold values from 0.25 to 1.5
Outputs:
- revised_outlook: float32 [4, 192, 64, 2048], P('member', None, 'lat', 'lon'), parts along dimension 0
There are 2 independent parts, one for each index of `member`. A program takes and returns all parts, laid end to end along the dimension named above; an argument that names none is the same for every part. Nothing has to cross between parts.
Inputs may be any that keep to these rules, and one draw needn't show every extreme that they name: `inflow_owner`: among the 16 rows of one device, no lon index appears more than 2 times. `outflow_owner`: among the 16 rows of one device, no lon index appears more than 2 times. `edge_sender`: No edge of the first lat index uses q = 0, none of the last uses q = 1.
All inputs are finite; a program needn't handle non-finite values.
Results may differ from a plain program's by a relative error of at most 0.0075.
Values may be sent and summed in bfloat16 or wider, within the bound.
A program may use at most 128 MiB of HBM per device.

v0:
```python
import jax
import jax.numpy as jnp
from jax import lax
from jax.sharding import PartitionSpec as P

BATCH_REALIZATION = 2
POINT_QUANTITIES = 192
PATCH_PARALLELS = 8
PATCH_MERIDIANS = 128
DSTEPS = 2
BLOCKS = 16
NODE_DEV = 256
HCAP = 48
HID = 512
LAYERS = 2


def extended_2(x, sides, width):
    for axis, dim in sides:
        size, length = (lax.axis_size(axis), x.shape[dim])
        up = [(i, (i + 1) % size) for i in range(size)]
        down = [(j, i) for i, j in up]
        last = lax.slice_in_dim(x, length - width, length, axis=dim)
        first = lax.slice_in_dim(x, 0, width, axis=dim)
        before = lax.ppermute(last, axis, up)
        after = lax.ppermute(first, axis, down)
        x = jnp.concatenate([before, x, after], axis=dim)
    return x


def with_halo(x, sides, width):
    edges = {}
    for axis, dim in sides:
        size, length = (lax.axis_size(axis), x.shape[dim])
        up = [(i, (i + 1) % size) for i in range(size)]
        last = lax.slice_in_dim(x, length - width, length, axis=dim)
        first = lax.slice_in_dim(x, 0, width, axis=dim)
        edges[dim] = (
            lax.ppermute(last, axis, up),
            lax.ppermute(first, axis, [(b, a) for a, b in up]),
        )
    done = []
    for _, dim in sides:
        low, high = edges[dim]
        around = [(width, width) if d in done else (0, 0) for d in range(x.ndim)]
        x = jnp.concatenate([jnp.pad(low, around), x, jnp.pad(high, around)], axis=dim)
        done.append(dim)
    return x


def advance(extended, east_rate, north_rate, spread):
    middle = extended[:, 1:-1, 1:-1]
    west_cells = extended[:, 1:-1, :-2]
    east_cells = extended[:, 1:-1, 2:]
    south_cells = extended[:, :-2, 1:-1]
    north_cells = extended[:, 2:, 1:-1]
    result = middle - jnp.maximum(east_rate, 0.0) * (middle - west_cells)
    result = result - jnp.minimum(east_rate, 0.0) * (east_cells - middle)
    result = result - jnp.maximum(north_rate, 0.0) * (middle - south_cells)
    result = result - jnp.minimum(north_rate, 0.0) * (north_cells - middle)
    return result + spread * (west_cells + east_cells + south_cells + north_cells - 4.0 * middle)


def mend_poles(extended, margin):
    lat_index = lax.axis_index("lat")
    lat_count = lax.axis_size("lat")
    height = extended.shape[1]
    first_row = extended[:, margin : margin + 1, :]
    last_row = extended[:, height - margin - 1 : height - margin, :]
    row_ids = lax.broadcasted_iota(jnp.int32, (1, height, 1), 1)
    extended = jnp.where((lat_index == 0) & (row_ids < margin), first_row, extended)
    extended = jnp.where(
        (lat_index == lat_count - 1) & (row_ids >= height - margin), last_row, extended
    )
    return extended


def normalize(values):
    scale = lax.rsqrt(jnp.mean(values * values, axis=-1, keepdims=True) + 1e-06)
    return (values * scale).astype(jnp.bfloat16)


def one_hot_rows(indices, first, count):
    targets = first + lax.broadcasted_iota(jnp.int32, (count, 1), 0)
    return (indices[None, :] == targets).astype(jnp.bfloat16)


def summed_into(values, indices, first, count):
    selector = one_hot_rows(indices, first, count)
    return jnp.dot(selector, values, preferred_element_type=jnp.float32)


def place_blocks(values, owners, targets, lon_count, capacity):
    owner_list = owners[:, 0]
    block_count = owner_list.shape[0]
    matches = (owner_list[:, None] == owner_list[None, :]).astype(jnp.int32)
    earlier = jnp.sum(jnp.tril(matches, -1), axis=1)
    slot_index = owner_list * capacity + earlier
    slot_count = lon_count * capacity
    hits = (slot_index[None, :] == jnp.arange(slot_count, dtype=jnp.int32)[:, None]).astype(
        jnp.int32
    )
    filled = jnp.sum(hits, axis=1) > 0
    source_block = jnp.sum(hits * jnp.arange(block_count, dtype=jnp.int32)[None, :], axis=1)
    packed = jnp.where(
        filled[:, None, None], jnp.take(values, source_block, axis=0), jnp.zeros((), values.dtype)
    )
    placed = jnp.where(filled[:, None], jnp.take(targets, source_block, axis=0), 0)
    return (packed, placed)


def body(
    fields,
    wind_east,
    wind_north,
    diffusion,
    inflow_owner,
    inflow_cell,
    inflow_node,
    inflow_weight,
    encoder,
    sender_weight,
    receiver_weight,
    update_weight,
    decoder,
    edge_sender,
    edge_receiver,
    halo_rows,
    outflow_owner,
    outflow_node,
    outflow_cell,
    outflow_weight,
):
    latent_quantities = BATCH_REALIZATION * POINT_QUANTITIES
    lon_count = lax.axis_size("lon")
    capacity = max(2, (2 * BLOCKS + lon_count - 1) // lon_count)
    current_condition = fields.reshape(latent_quantities, PATCH_PARALLELS, PATCH_MERIDIANS)
    stacked = jnp.concatenate(
        [current_condition, wind_east[None], wind_north[None], diffusion[None]], axis=0
    )
    extended = extended_2(stacked, (("lat", 1), ("lon", 2)), DSTEPS)
    current_condition = extended[:latent_quantities]
    rates = extended[latent_quantities:]
    for sub_step in range(DSTEPS):
        margin = DSTEPS - sub_step
        current_condition = mend_poles(current_condition, margin)
        offset = sub_step + 1
        window = rates[:, offset : rates.shape[1] - offset, offset : rates.shape[2] - offset]
        current_condition = advance(current_condition, window[0], window[1], window[2])
    table = current_condition.reshape(latent_quantities, PATCH_PARALLELS * PATCH_MERIDIANS)
    picked = jnp.take(table, inflow_cell.reshape(-1), axis=1)
    inflow = (picked.T * inflow_weight.reshape(-1, 1)).astype(jnp.bfloat16)
    packed, placed = place_blocks(
        inflow.reshape(BLOCKS, -1, latent_quantities),
        inflow_owner,
        inflow_node,
        lon_count,
        capacity,
    )
    arrived, arrived_nodes = (
        lax.all_to_all(packed, "lon", split_axis=0, concat_axis=0, tiled=True),
        lax.all_to_all(placed, "lon", split_axis=0, concat_axis=0, tiled=True),
    )
    node_input = summed_into(
        arrived.reshape(-1, latent_quantities), arrived_nodes.reshape(-1), 0, NODE_DEV
    )
    embedded = node_input.astype(jnp.bfloat16).reshape(
        NODE_DEV * BATCH_REALIZATION, POINT_QUANTITIES
    )
    hidden = jax.nn.silu(jnp.dot(embedded, encoder, preferred_element_type=jnp.float32))
    senders = edge_sender.reshape(-1)
    receivers = edge_receiver.reshape(-1)
    wanted = halo_rows.reshape(4, HCAP)
    gather_table = one_hot_rows(receivers, 0, NODE_DEV)
    for layer in range(LAYERS):
        normed = normalize(hidden)
        source = (
            jnp.dot(normed, sender_weight[layer], preferred_element_type=jnp.float32)
            .astype(jnp.bfloat16)
            .reshape(NODE_DEV, BATCH_REALIZATION, HID)
        )
        target = jnp.dot(
            normed, receiver_weight[layer], preferred_element_type=jnp.float32
        ).reshape(NODE_DEV, BATCH_REALIZATION, HID)
        arrived = with_halo(source[None, None], (("lat", 0), ("lon", 1)), 1)
        borrowed = jnp.stack(
            [
                jnp.take(arrived[0, 1], wanted[0], axis=0),
                jnp.take(arrived[2, 1], wanted[1], axis=0),
                jnp.take(arrived[1, 0], wanted[2], axis=0),
                jnp.take(arrived[1, 2], wanted[3], axis=0),
            ],
            axis=0,
        )
        lookup = jnp.concatenate(
            [source, borrowed.reshape(4 * HCAP, BATCH_REALIZATION, HID)], axis=0
        )
        summed_terms = jnp.take(lookup, senders, axis=0).astype(jnp.float32) + jnp.take(
            target, receivers, axis=0
        )
        message = (
            jax.nn.silu(summed_terms).astype(jnp.bfloat16).reshape(-1, BATCH_REALIZATION * HID)
        )
        collected = jnp.dot(gather_table, message, preferred_element_type=jnp.float32).astype(
            jnp.bfloat16
        )
        hidden = hidden + jnp.dot(
            collected.reshape(NODE_DEV * BATCH_REALIZATION, HID),
            update_weight[layer],
            preferred_element_type=jnp.float32,
        )
    correction = (
        jnp.dot(normalize(hidden), decoder, preferred_element_type=jnp.float32)
        .astype(jnp.bfloat16)
        .reshape(NODE_DEV, latent_quantities)
    )
    chosen = jnp.take(correction, outflow_node.reshape(-1), axis=0)
    outflow = (chosen.astype(jnp.float32) * outflow_weight.reshape(-1, 1)).astype(jnp.bfloat16)
    packed, placed = place_blocks(
        outflow.reshape(BLOCKS, -1, latent_quantities),
        outflow_owner,
        outflow_cell,
        lon_count,
        capacity,
    )
    arrived, arrived_cells = (
        lax.all_to_all(packed, "lon", split_axis=0, concat_axis=0, tiled=True),
        lax.all_to_all(placed, "lon", split_axis=0, concat_axis=0, tiled=True),
    )
    cell_count = PATCH_PARALLELS * PATCH_MERIDIANS
    cell_ids = lax.broadcasted_iota(jnp.int32, (1, cell_count), 1)
    landing = (arrived_cells.reshape(-1)[:, None] == cell_ids).astype(jnp.bfloat16)
    add_learned_fix = lax.dot_general(
        arrived.reshape(-1, latent_quantities),
        landing,
        (((0,), (0,)), ((), ())),
        preferred_element_type=jnp.float32,
    )
    revised_outlook = current_condition + add_learned_fix.reshape(
        latent_quantities, PATCH_PARALLELS, PATCH_MERIDIANS
    )
    return revised_outlook.reshape(
        BATCH_REALIZATION, POINT_QUANTITIES, PATCH_PARALLELS, PATCH_MERIDIANS
    )


def solution(mesh):
    placed = (
        P("member", None, "lat", "lon"),
        P("lat", "lon"),
        P("lat", "lon"),
        P("lat", "lon"),
        P(("lat", "lon"), None),
        P(("lat", "lon"), None),
        P(("lat", "lon"), None),
        P(("lat", "lon"), None),
        P(),
        P(),
        P(),
        P(),
        P(),
        P("lat", "lon", None),
        P("lat", "lon", None),
        P("lat", "lon", None, None),
        P(("lat", "lon"), None),
        P(("lat", "lon"), None),
        P(("lat", "lon"), None),
        P(("lat", "lon"), None),
    )
    return jax.shard_map(
        body, mesh=mesh, in_specs=placed, out_specs=P("member", None, "lat", "lon"), check_vma=False
    )
```

profile of v0, /device:TPU:2, one launch (start us, length us, event | category | flops | bytes accessed | tf_op | source)
XLA Modules:
  0.0 388.2 jit_solution(7057526689188279259)
XLA Ops:
  5.3 11.2 %all-to-all-start = ((s32[16,2,128]{2,1,0:T(2,128)}), s32[16,2,128]{2,1,0:T(2,128)S(1)}, u32[]{:S(2)}, u32[]{:S(2)}) async-start(s32[16,2,128]{2,1,0:T(2,128)} %bitcast.10), calls=%async_computation | async-start | bytes 32768 | tf_op jit(solution)/shard_map/all_to_all | solution.py:162
  16.8 3.0 fusion.44
  19.8 2.6 copy.71
  22.4 3.5 collective-permute-start.2
  25.8 2.6 copy.72
  28.4 2.3 collective-permute-start.3
  30.7 2.3 copy.73
  34.1 2.2 copy.74
  36.2 9.2 %pad_maximum_fusion = f32[387,12,132]{2,0,1:T(8,128)S(1)} fusion(f32[387,12,2]{2,0,1:T(8,128)} %copy.74, f32[387,2,128]{2,0,1:T(8,128)S(1)} %collective-permute-done.1, f32[1,8,128]{2,0,1:T(1,128)S(1)} %bitcast.140, f32[1,8,128]{2,0,1:T(1,128)S(1)} %bitcast.143, f32[1,8,128]{2,0,1:T(1,128)S(1)} %bitcast.146, f32[384,8,128]{2,0,1:T(8,128)S(1)} %bitcast.127, ...), kind=kLoop, calls=%fused_computation.28 | loop fusion | flops 4291056 | bytes 4904064 | tf_op jit(solution)/shard_map/concatenate | solution.py:27
  46.3 4.3 %multiply_add_fusion = f32[384,10,130]{2,0,1:T(8,128)S(1)} fusion(f32[384,12,132]{2,0,1:T(8,128)S(1)} %fusion.6, f32[10,130]{1,0:T(8,128)S(1)} %get-tuple-element.55, f32[10,130]{1,0:T(8,128)S(1)} %get-tuple-element.56, f32[10,130]{1,0:T(8,128)S(1)} %get-tuple-element.57, f32[10,130]{1,0:T(8,128)S(1)} %get-tuple-element.58, f32[10,130]{1,0:T(8,128)S(1)} %bitcast.136), kind=kLoop, calls=%fused_computation.34 | loop fusion | flops 9484800 | bytes 12006800 | tf_op jit(solution)/shard_map/add | solution.py:61
  50.6 4.3 %select_select_fusion = f32[384,10,130]{2,0,1:T(8,128)S(1)} fusion(f32[384,130]{1,0:T(8,128)S(1)} %get-tuple-element.32, f32[384,130]{1,0:T(8,128)S(1)} %get-tuple-element.31, pred[10]{0:T(512)(128)(4,1)S(1)} %get-tuple-element.59, pred[10]{0:T(512)(128)(4,1)S(1)} %get-tuple-element.60, f32[10,130]{1,0:T(8,128)S(1)} %get-tuple-element.55, ...), kind=kLoop, calls=%fused_computation.33 | loop fusion | flops 10483200 | bytes 12406180 | tf_op jit(solution)/shard_map/jit(_where)/select_n | solution.py:72
  57.2 8.8 %gather_fusion = f32[2048,384]{1,0:T(8,128)} fusion(f32[384,1024]{0,1:T(8,128)S(1)} %bitcast.124, s32[2048]{0:T(1024)S(1)} %broadcast_clamp_fusion.1), kind=kCustom, calls=%fused_computation.16 | custom fusion | bytes 6299648 | tf_op jit(solution)/shard_map/jit(_take)/gather | solution.py:151
  66.0 2.4 multiply_convert_fusion.2
  68.4 2.6 gather_fusion.3
  71.0 4.1 %select_select_fusion.2 = bf16[32,128,384]{2,1,0:T(8,128)(2,1)} fusion(bf16[32,128,384]{2,1,0:T(8,128)(2,1)} %gather_fusion.3, pred[32]{0:T(512)(128)(4,1)S(1)} %compare_and_fusion.9, pred[32]{0:T(512)(128)(4,1)S(1)} %broadcast_compare_fusion), kind=kLoop, calls=%fused_computation.38 | loop fusion | flops 3145728 | bytes 6291520 | tf_op jit(solution)/shard_map/jit(_where)/select_n | solution.py:105
  75.7 8.9 %all-to-all-start.1 = ((bf16[32,128,384]{2,1,0:T(8,128)(2,1)}), bf16[32,128,384]{2,1,0:T(8,128)(2,1)S(1)}, u32[]{:S(2)}, u32[]{:S(2)}) async-start(bf16[32,128,384]{2,1,0:T(8,128)(2,1)} %select_select_fusion.2), calls=%async_computation.1 | async-start | bytes 6291456 | tf_op jit(solution)/shard_map/all_to_all | solution.py:161
  89.7 67.7 %all-to-all-done.1 = bf16[32,128,384]{2,1,0:T(8,128)(2,1)S(1)} async-done(((bf16[32,128,384]{2,1,0:T(8,128)(2,1)}), bf16[32,128,384]{2,1,0:T(8,128)(2,1)S(1)}, u32[]{:S(2)}, u32[]{:S(2)}) %all-to-all-start.1) | async-done | bytes 3145760 | tf_op jit(solution)/shard_map/all_to_all | solution.py:161
  157.4 4.1 %all-to-all-start.3 = ((s32[16,2,128]{2,1,0:T(2,128)}), s32[16,2,128]{2,1,0:T(2,128)}, u32[]{:S(2)}, u32[]{:S(2)}) async-start(s32[16,2,128]{2,1,0:T(2,128)} %bitcast.56), calls=%async_computation.3 | async-start | bytes 32768 | tf_op jit(solution)/shard_map/all_to_all | solution.py:228
  161.5 2.0 fusion.16
  167.8 3.2 collective-permute-start.6
  171.1 2.5 collective-permute-start.7
  175.2 10.1 %gather_fusion.9 = f32[1536,2,512]{2,1,0:T(2,128)} fusion(f32[256,2,512]{2,1,0:T(2,128)S(1)} %copy.78, s32[2048]{0:T(1024)S(1)} %pad_clamp_fusion), kind=kCustom, calls=%fused_computation.4.clone | custom fusion | bytes 12589056 | tf_op jit(solution)/shard_map/jit(_take)/gather | solution.py:198
  185.3 1.9 gather_fusion.4
  187.5 1.9 gather_fusion.5
  189.4 4.0 %collective-permute-done.6 = bf16[1,1,256,2,512]{4,3,2,1,0:T(2,128)(2,1)} collective-permute-done((bf16[1,1,256,2,512]{4,3,2,1,0:T(2,128)(2,1)S(1)}, bf16[1,1,256,2,512]{4,3,2,1,0:T(2,128)(2,1)}, u32[]{:S(2)}, u32[]{:S(2)}) %collective-permute-start.6) | collective-permute-done | bytes 524320 | tf_op jit(solution)/shard_map/ppermute | solution.py:39
  193.4 1.8 gather_fusion.6
  200.4 9.6 %gather_fusion.8 = bf16[1536,2,512]{2,1,0:T(2,128)(2,1)} fusion(bf16[448,2,512]{2,1,0:T(2,128)(2,1)S(1)} %pad_maximum_fusion.2, s32[2048]{0:T(1024)S(1)} %pad_clamp_fusion.1), kind=kCustom, calls=%fused_computation.3.clone | custom fusion | bytes 6297600 | tf_op jit(solution)/shard_map/jit(_take)/gather | solution.py:198
  210.0 6.5 %multiply_convert_fusion.1 = bf16[1536,2,512]{2,0,1:T(8,128)(2,1)S(1)} fusion(f32[1536,2,512]{2,1,0:T(2,128)} %gather_fusion.9, bf16[1536,2,512]{2,1,0:T(2,128)(2,1)} %gather_fusion.8, pred[1536]{0:T(1024)(128)(4,1)S(1)} %copy-done.24, pred[1536]{0:T(1024)(128)(4,1)S(1)} %copy-done.25), kind=kLoop, calls=%fused_computation.27 | loop fusion | flops 14155776 | bytes 12585984 | tf_op jit(solution)/shard_map/convert_element_type | solution.py:202
  216.5 2.8 copy.80
  219.3 3.1 fusion.14
  227.3 3.2 collective-permute-start.10
  231.1 2.8 collective-permute-start.11
  235.6 9.9 %gather_fusion.15 = f32[1536,2,512]{2,1,0:T(2,128)} fusion(f32[256,2,512]{2,1,0:T(2,128)S(1)} %copy.83, s32[2048]{0:T(1024)S(1)} %pad_clamp_fusion), kind=kCustom, calls=%fused_computation.15.clone | custom fusion | bytes 12589056 | tf_op jit(solution)/shard_map/jit(_take)/gather | solution.py:198
  245.4 1.9 gather_fusion.10
  247.6 1.9 gather_fusion.11
  249.5 2.4 collective-permute-done.10
  251.9 1.8 gather_fusion.12
  258.8 9.6 %gather_fusion.14 = bf16[1536,2,512]{2,1,0:T(2,128)(2,1)} fusion(bf16[448,2,512]{2,1,0:T(2,128)(2,1)S(1)} %pad_maximum_fusion.3, s32[2048]{0:T(1024)S(1)} %pad_clamp_fusion.1), kind=kCustom, calls=%fused_computation.14.clone | custom fusion | bytes 6297600 | tf_op jit(solution)/shard_map/jit(_take)/gather | solution.py:198
  268.5 6.5 %multiply_convert_fusion = bf16[1536,2,512]{2,0,1:T(8,128)(2,1)S(1)} fusion(f32[1536,2,512]{2,1,0:T(2,128)} %gather_fusion.15, bf16[1536,2,512]{2,1,0:T(2,128)(2,1)} %gather_fusion.14, pred[1536]{0:T(1024)(128)(4,1)S(1)} %copy-done.24, pred[1536]{0:T(1024)(128)(4,1)S(1)} %copy-done.25), kind=kLoop, calls=%fused_computation.26 | loop fusion | flops 14155776 | bytes 12585984 | tf_op jit(solution)/shard_map/convert_element_type | solution.py:202
  275.0 2.8 copy.85
  277.8 3.0 fusion.15
  282.5 7.5 %gather_fusion.1 = bf16[2048,384]{1,0:T(8,128)(2,1)S(1)} fusion(bf16[256,384]{1,0:T(8,128)(2,1)S(1)} %reshape.316, s32[2048]{0:T(1024)S(1)} %copy-done.18), kind=kCustom, calls=%fused_computation.17 | custom fusion | bytes 3153920 | tf_op jit(solution)/shard_map/jit(_take)/gather | solution.py:217
  290.9 2.7 gather_fusion.16
  293.7 4.1 %select_select_fusion.1 = bf16[32,128,384]{2,1,0:T(8,128)(2,1)} fusion(bf16[32,128,384]{2,1,0:T(8,128)(2,1)} %gather_fusion.16, pred[32]{0:T(512)(128)(4,1)S(1)} %copy-done.43, pred[32]{0:T(512)(128)(4,1)S(1)} %copy-done.45), kind=kLoop, calls=%fused_computation.37 | loop fusion | flops 3145728 | bytes 6291520 | tf_op jit(solution)/shard_map/jit(_where)/select_n | solution.py:105
  297.7 9.7 %all-to-all-start.2 = ((bf16[32,128,384]{2,1,0:T(8,128)(2,1)}), bf16[32,128,384]{2,1,0:T(8,128)(2,1)}, u32[]{:S(2)}, u32[]{:S(2)}) async-start(bf16[32,128,384]{2,1,0:T(8,128)(2,1)} %select_select_fusion.1), calls=%async_computation.2 | async-start | bytes 6291456 | tf_op jit(solution)/shard_map/all_to_all | solution.py:227
  307.4 73.0 %all-to-all-done.2 = bf16[32,128,384]{2,1,0:T(8,128)(2,1)} async-done(((bf16[32,128,384]{2,1,0:T(8,128)(2,1)}), bf16[32,128,384]{2,1,0:T(8,128)(2,1)}, u32[]{:S(2)}, u32[]{:S(2)}) %all-to-all-start.2) | async-done | bytes 3145760 | tf_op jit(solution)/shard_map/all_to_all | solution.py:227
  380.4 5.5 %fusion.11 = f32[384,8,128]{2,0,1:T(8,128)S(1)} fusion(f32[384,8,128]{2,0,1:T(8,128)S(1)} %copy-done.5, bf16[4096,384,1]{1,0,2:T(8,128)(2,1)} %bitcast.64, s32[8,128]{1,0:T(8,128)S(1)} %multiply_add_fusion.2, s32[4096]{0:T(1024)} %bitcast.57), kind=kOutput, calls=%fused_computation.49 | convolution fusion | flops 3225812992 | bytes 6311936 | tf_op jit(solution)/shard_map/dot_general | solution.py:233
  385.9 2.1 copy.89
  (206 shorter events, 41.1 us)
Async XLA Ops:
  0.0 163.7 %copy-start = (bf16[192,512]{1,0:T(8,128)(2,1)S(1)}, bf16[192,512]{1,0:T(8,128)(2,1)}, u32[]{:S(2)}) copy-start(bf16[192,512]{1,0:T(8,128)(2,1)} %param.38) | copy-start | bytes 589828
  0.0 3.7 copy-start.37
  0.0 3.7 copy-start.38
  0.0 4.0 %copy-start.8 = (s32[16,128]{1,0:T(8,128)S(1)}, s32[16,128]{1,0:T(8,128)}, u32[]{:S(2)}) copy-start(s32[16,128]{1,0:T(8,128)} %param.36) | copy-start | bytes 24580
  0.1 16.5 %copy-start.19 = (s32[16,128]{1,0:T(8,128)S(1)}, s32[16,128]{1,0:T(8,128)}, u32[]{:S(2)}) copy-start(s32[16,128]{1,0:T(8,128)} %param.35) | copy-start | bytes 24580
  2.0 14.7 %collective-permute-start = (f32[387,2,128]{2,0,1:T(8,128)S(1)}, f32[387,2,128]{2,0,1:T(8,128)S(1)}, u32[]{:S(2)}, u32[]{:S(2)}) collective-permute-start(f32[387,2,128]{2,0,1:T(8,128)S(1)} %get-tuple-element.35), channel_id=1, source_target_pairs={{0,16},{16,32},{32,48},{48,64},{64,80},{80,96},{96,112},{112,0},{1... | collective-permute-start | bytes 1188872 | tf_op jit(solution)/shard_map/ppermute | solution.py:25
  2.0 14.6 %collective-permute-start.1 = (f32[387,2,128]{2,0,1:T(8,128)S(1)}, f32[387,2,128]{2,0,1:T(8,128)S(1)}, u32[]{:S(2)}, u32[]{:S(2)}) collective-permute-start(f32[387,2,128]{2,0,1:T(8,128)S(1)} %get-tuple-element.36), channel_id=1, source_target_pairs={{16,0},{32,16},{48,32},{64,48},{80,64},{96,80},{112,96},{0,112},{1... | collective-permute-start | bytes 1188872 | tf_op jit(solution)/shard_map/ppermute | solution.py:26
  5.3 69.8 %all-to-all-start = ((s32[16,2,128]{2,1,0:T(2,128)}), s32[16,2,128]{2,1,0:T(2,128)S(1)}, u32[]{:S(2)}, u32[]{:S(2)}) async-start(s32[16,2,128]{2,1,0:T(2,128)} %bitcast.10), calls=%async_computation | async-start | bytes 32768 | tf_op jit(solution)/shard_map/all_to_all | solution.py:162
  22.4 8.3 %collective-permute-start.2 = (f32[387,12,2]{0,2,1:T(2,128)S(1)}, f32[387,12,2]{0,2,1:T(2,128)S(1)}, u32[]{:S(2)}, u32[]{:S(2)}) collective-permute-start(f32[387,12,2]{0,2,1:T(2,128)S(1)} %copy.71), channel_id=1, source_target_pairs={{0,1},{1,2},{2,3},{3,4},{4,5},{5,6},{6,7},{7,8},{8,9},{9,10},{10,1... | collective-permute-start | bytes 111464 | tf_op jit(solution)/shard_map/ppermute | solution.py:25
  28.4 5.6 %collective-permute-start.3 = (f32[387,12,2]{0,2,1:T(2,128)S(1)}, f32[387,12,2]{0,2,1:T(2,128)S(1)}, u32[]{:S(2)}, u32[]{:S(2)}) collective-permute-start(f32[387,12,2]{0,2,1:T(2,128)S(1)} %copy.72), channel_id=1, source_target_pairs={{1,0},{2,1},{3,2},{4,3},{5,4},{6,5},{7,6},{8,7},{9,8},{10,9},{11,1... | collective-permute-start | bytes 111464 | tf_op jit(solution)/shard_map/ppermute | solution.py:26
  56.7 9.3 %copy-start.4 = (f32[384,8,128]{2,0,1:T(8,128)}, f32[384,8,128]{2,0,1:T(8,128)S(1)}, u32[]{:S(2)}) copy-start(f32[384,8,128]{2,0,1:T(8,128)S(1)} %multiply_add_fusion.1) | copy-start | bytes 4718596
  57.2 8.8 %copy-start.27 = (f32[16,128]{1,0:T(8,128)S(1)}, f32[16,128]{1,0:T(8,128)}, u32[]{:S(2)}) copy-start(f32[16,128]{1,0:T(8,128)} %param.37) | copy-start | bytes 24580
  75.1 9.5 %copy-start.31 = (s32[1,1,1536]{2,1,0:T(1,128)S(1)}, s32[1,1,1536]{2,1,0:T(1,128)}, u32[]{:S(2)}) copy-start(s32[1,1,1536]{2,1,0:T(1,128)} %param.43) | copy-start | bytes 18436
  75.1 9.5 %copy-start.32 = (s32[1,1,1536]{2,1,0:T(1,128)S(1)}, s32[1,1,1536]{2,1,0:T(1,128)}, u32[]{:S(2)}) copy-start(s32[1,1,1536]{2,1,0:T(1,128)} %param.44) | copy-start | bytes 18436
  75.1 9.7 %copy-start.9 = (s32[16,128]{1,0:T(8,128)S(1)}, s32[16,128]{1,0:T(8,128)}, u32[]{:S(2)}) copy-start(s32[16,128]{1,0:T(8,128)} %param.48) | copy-start | bytes 24580
  75.1 10.3 %copy-start.39 = (s32[1,1,4,48]{3,2,1,0:T(4,128)S(1)}, s32[1,1,4,48]{3,2,1,0:T(4,128)}, u32[]{:S(2)}) copy-start(s32[1,1,4,48]{3,2,1,0:T(4,128)} %param.45) | copy-start | bytes 2308
  75.1 14.0 %copy-start.20 = (s32[16,128]{1,0:T(8,128)S(1)}, s32[16,128]{1,0:T(8,128)}, u32[]{:S(2)}) copy-start(s32[16,128]{1,0:T(8,128)} %param.47) | copy-start | bytes 24580
  75.7 81.6 %all-to-all-start.1 = ((bf16[32,128,384]{2,1,0:T(8,128)(2,1)}), bf16[32,128,384]{2,1,0:T(8,128)(2,1)S(1)}, u32[]{:S(2)}, u32[]{:S(2)}) async-start(bf16[32,128,384]{2,1,0:T(8,128)(2,1)} %select_select_fusion.2), calls=%async_computation.1 | async-start | bytes 6291456 | tf_op jit(solution)/shard_map/all_to_all | solution.py:161
  84.8 76.7 %copy-start.30 = (s32[1024]{0:T(1024)}, s32[1024]{0:T(1024)S(1)}, u32[]{:S(2)}) copy-start(s32[1024]{0:T(1024)S(1)} %pad_clamp_fusion.2) | copy-start | bytes 12292
  87.2 74.3 %copy-start.42 = (pred[32]{0:T(512)(128)(4,1)}, pred[32]{0:T(512)(128)(4,1)S(1)}, u32[]{:S(2)}) copy-start(pred[32]{0:T(512)(128)(4,1)S(1)} %compare_and_fusion.4) | copy-start | bytes 100
  87.2 74.3 %copy-start.44 = (pred[32]{0:T(512)(128)(4,1)}, pred[32]{0:T(512)(128)(4,1)S(1)}, u32[]{:S(2)}) copy-start(pred[32]{0:T(512)(128)(4,1)S(1)} %broadcast_compare_fusion.1) | copy-start | bytes 100
  157.4 140.4 %all-to-all-start.3 = ((s32[16,2,128]{2,1,0:T(2,128)}), s32[16,2,128]{2,1,0:T(2,128)}, u32[]{:S(2)}, u32[]{:S(2)}) async-start(s32[16,2,128]{2,1,0:T(2,128)} %bitcast.56), calls=%async_computation.3 | async-start | bytes 32768 | tf_op jit(solution)/shard_map/all_to_all | solution.py:228
  164.2 6.8 %copy-start.40 = (s32[48]{0:T(128)S(1)}, s32[48]{0:T(128)}, u32[]{:S(2)}) copy-start(s32[48]{0:T(128)} %get-tuple-element.44) | copy-start | bytes 580
  165.2 8.7 %copy-start.10 = (bf16[2,512,512]{2,1,0:T(8,128)(2,1)S(1)}, bf16[2,512,512]{2,1,0:T(8,128)(2,1)}, u32[]{:S(2)}) copy-start(bf16[2,512,512]{2,1,0:T(8,128)(2,1)} %param.40) | copy-start | bytes 3145732
  166.0 19.3 %collective-permute-start.4 = (bf16[1,1,256,2,512]{4,3,2,1,0:T(2,128)(2,1)S(1)}, bf16[1,1,256,2,512]{4,3,2,1,0:T(2,128)(2,1)}, u32[]{:S(2)}, u32[]{:S(2)}) collective-permute-start(bf16[1,1,256,2,512]{4,3,2,1,0:T(2,128)(2,1)S(1)} %broadcast_in_dim_reshape.4), channel_id=1, source_target_pairs={{0,16},{16,32},{32,48},{48,64},{64,80},{80,96},{96,112},{112,0},{1... | collective-permute-start | bytes 1572872 | tf_op jit(solution)/shard_map/ppermute | solution.py:39
  166.1 21.4 %collective-permute-start.5 = (bf16[1,1,256,2,512]{4,3,2,1,0:T(2,128)(2,1)S(1)}, bf16[1,1,256,2,512]{4,3,2,1,0:T(2,128)(2,1)}, u32[]{:S(2)}, u32[]{:S(2)}) collective-permute-start(bf16[1,1,256,2,512]{4,3,2,1,0:T(2,128)(2,1)S(1)} %broadcast_in_dim_reshape.4), channel_id=1, source_target_pairs={{16,0},{32,16},{48,32},{64,48},{80,64},{96,80},{112,96},{0,112},{1... | collective-permute-start | bytes 1572872 | tf_op jit(solution)/shard_map/ppermute | solution.py:40
  167.8 25.6 %collective-permute-start.6 = (bf16[1,1,256,2,512]{4,3,2,1,0:T(2,128)(2,1)S(1)}, bf16[1,1,256,2,512]{4,3,2,1,0:T(2,128)(2,1)}, u32[]{:S(2)}, u32[]{:S(2)}) collective-permute-start(bf16[1,1,256,2,512]{4,3,2,1,0:T(2,128)(2,1)S(1)} %broadcast_in_dim_reshape.4), channel_id=1, source_target_pairs={{0,1},{1,2},{2,3},{3,4},{4,5},{5,6},{6,7},{7,8},{8,9},{9,10},{10,1... | collective-permute-start | bytes 1572872 | tf_op jit(solution)/shard_map/ppermute | solution.py:39
  171.1 25.4 %collective-permute-start.7 = (bf16[1,1,256,2,512]{4,3,2,1,0:T(2,128)(2,1)S(1)}, bf16[1,1,256,2,512]{4,3,2,1,0:T(2,128)(2,1)}, u32[]{:S(2)}, u32[]{:S(2)}) collective-permute-start(bf16[1,1,256,2,512]{4,3,2,1,0:T(2,128)(2,1)S(1)} %broadcast_in_dim_reshape.4), channel_id=1, source_target_pairs={{1,0},{2,1},{3,2},{4,3},{5,4},{6,5},{7,6},{8,7},{9,8},{10,9},{11,1... | collective-permute-start | bytes 1572872 | tf_op jit(solution)/shard_map/ppermute | solution.py:40
  175.2 12.1 %copy-start.36 = (pred[48]{0:T(512)(128)(4,1)S(1)}, pred[48]{0:T(512)(128)(4,1)}, u32[]{:S(2)}) copy-start(pred[48]{0:T(512)(128)(4,1)} %get-tuple-element.16) | copy-start | bytes 148
  175.2 20.0 %copy-start.35 = (pred[48]{0:T(512)(128)(4,1)S(1)}, pred[48]{0:T(512)(128)(4,1)}, u32[]{:S(2)}) copy-start(pred[48]{0:T(512)(128)(4,1)} %get-tuple-element.41) | copy-start | bytes 148
  175.2 20.2 %copy-start.34 = (pred[48]{0:T(512)(128)(4,1)S(1)}, pred[48]{0:T(512)(128)(4,1)}, u32[]{:S(2)}) copy-start(pred[48]{0:T(512)(128)(4,1)} %get-tuple-element.45) | copy-start | bytes 148
  175.2 23.0 %copy-start.33 = (pred[48]{0:T(512)(128)(4,1)S(1)}, pred[48]{0:T(512)(128)(4,1)}, u32[]{:S(2)}) copy-start(pred[48]{0:T(512)(128)(4,1)} %get-tuple-element.43) | copy-start | bytes 148
  200.3 9.7 %copy-start.24 = (pred[1536]{0:T(1024)(128)(4,1)S(1)}, pred[1536]{0:T(1024)(128)(4,1)}, u32[]{:S(2)}) copy-start(pred[1536]{0:T(1024)(128)(4,1)} %get-tuple-element.65) | copy-start | bytes 4612
  200.3 9.7 %copy-start.25 = (pred[1536]{0:T(1024)(128)(4,1)S(1)}, pred[1536]{0:T(1024)(128)(4,1)}, u32[]{:S(2)}) copy-start(pred[1536]{0:T(1024)(128)(4,1)} %get-tuple-element.66) | copy-start | bytes 4612
  219.3 3.3 copy-start.12
  222.6 7.9 %copy-start.21 = (s32[16,128]{1,0:T(8,128)S(1)}, s32[16,128]{1,0:T(8,128)}, u32[]{:S(2)}) copy-start(s32[16,128]{1,0:T(8,128)} %param.47) | copy-start | bytes 24580
  224.1 10.2 %copy-start.11 = (bf16[2,512,512]{2,1,0:T(8,128)(2,1)S(1)}, bf16[2,512,512]{2,1,0:T(8,128)(2,1)}, u32[]{:S(2)}) copy-start(bf16[2,512,512]{2,1,0:T(8,128)(2,1)} %param.40) | copy-start | bytes 3145732
  224.9 20.5 %collective-permute-start.8 = (bf16[1,1,256,2,512]{4,3,2,1,0:T(2,128)(2,1)S(1)}, bf16[1,1,256,2,512]{4,3,2,1,0:T(2,128)(2,1)}, u32[]{:S(2)}, u32[]{:S(2)}) collective-permute-start(bf16[1,1,256,2,512]{4,3,2,1,0:T(2,128)(2,1)S(1)} %broadcast_in_dim_reshape.10), channel_id=1, source_target_pairs={{0,16},{16,32},{32,48},{48,64},{64,80},{80,96},{96,112},{112,0},{1... | collective-permute-start | bytes 1572872 | tf_op jit(solution)/shard_map/ppermute | solution.py:39
  225.5 22.0 %collective-permute-start.9 = (bf16[1,1,256,2,512]{4,3,2,1,0:T(2,128)(2,1)S(1)}, bf16[1,1,256,2,512]{4,3,2,1,0:T(2,128)(2,1)}, u32[]{:S(2)}, u32[]{:S(2)}) collective-permute-start(bf16[1,1,256,2,512]{4,3,2,1,0:T(2,128)(2,1)S(1)} %broadcast_in_dim_reshape.10), channel_id=1, source_target_pairs={{16,0},{32,16},{48,32},{64,48},{80,64},{96,80},{112,96},{0,112},{1... | collective-permute-start | bytes 1572872 | tf_op jit(solution)/shard_map/ppermute | solution.py:40
  227.3 24.6 %collective-permute-start.10 = (bf16[1,1,256,2,512]{4,3,2,1,0:T(2,128)(2,1)S(1)}, bf16[1,1,256,2,512]{4,3,2,1,0:T(2,128)(2,1)}, u32[]{:S(2)}, u32[]{:S(2)}) collective-permute-start(bf16[1,1,256,2,512]{4,3,2,1,0:T(2,128)(2,1)S(1)} %broadcast_in_dim_reshape.10), channel_id=1, source_target_pairs={{0,1},{1,2},{2,3},{3,4},{4,5},{5,6},{6,7},{7,8},{8,9},{9,10},{10,1... | collective-permute-start | bytes 1572872 | tf_op jit(solution)/shard_map/ppermute | solution.py:39
  231.1 23.8 %collective-permute-start.11 = (bf16[1,1,256,2,512]{4,3,2,1,0:T(2,128)(2,1)S(1)}, bf16[1,1,256,2,512]{4,3,2,1,0:T(2,128)(2,1)}, u32[]{:S(2)}, u32[]{:S(2)}) collective-permute-start(bf16[1,1,256,2,512]{4,3,2,1,0:T(2,128)(2,1)S(1)} %broadcast_in_dim_reshape.10), channel_id=1, source_target_pairs={{1,0},{2,1},{3,2},{4,3},{5,4},{6,5},{7,6},{8,7},{9,8},{10,9},{11,1... | collective-permute-start | bytes 1572872 | tf_op jit(solution)/shard_map/ppermute | solution.py:40
  277.8 3.3 copy-start.3
  277.8 3.3 copy-start.13
  282.5 7.5 %copy-start.28 = (f32[16,128]{1,0:T(8,128)S(1)}, f32[16,128]{1,0:T(8,128)}, u32[]{:S(2)}) copy-start(f32[16,128]{1,0:T(8,128)} %param.49) | copy-start | bytes 24580
  282.5 7.5 %copy-start.29 = (pred[16,128]{1,0:T(8,128)(4,1)S(1)}, pred[16,128]{1,0:T(8,128)(4,1)}, u32[]{:S(2)}) copy-start(pred[16,128]{1,0:T(8,128)(4,1)} %compare_and_fusion.3) | copy-start | bytes 6148
  297.7 82.7 %copy-start.5 = (f32[384,8,128]{2,0,1:T(8,128)S(1)}, f32[384,8,128]{2,0,1:T(8,128)}, u32[]{:S(2)}) copy-start(f32[384,8,128]{2,0,1:T(8,128)} %copy-done.4) | copy-start | bytes 4718596
  297.7 82.7 %all-to-all-start.2 = ((bf16[32,128,384]{2,1,0:T(8,128)(2,1)}), bf16[32,128,384]{2,1,0:T(8,128)(2,1)}, u32[]{:S(2)}, u32[]{:S(2)}) async-start(bf16[32,128,384]{2,1,0:T(8,128)(2,1)} %select_select_fusion.1), calls=%async_computation.2 | async-start | bytes 6291456 | tf_op jit(solution)/shard_map/all_to_all | solution.py:227
  380.4 7.6 %copy-start.1 = (bf16[192,512]{1,0:T(8,128)(2,1)S(1)}, bf16[192,512]{1,0:T(8,128)(2,1)}, u32[]{:S(2)}) copy-start(bf16[192,512]{1,0:T(8,128)(2,1)} %param.38) | copy-start | bytes 589828
  (16 other events, 28.8 us)
where the time goes:
time: 394 us; the launch traced here: 388 us
  waiting for transfers between devices  150 us (38%)
  local copies, waits for them, and re-layouts  106 us (27%)
  other arithmetic  57 us (14%)
  starting transfers between devices  56.5 us (14%)
  matrix products  17.3 us (4%)
    all_to_all x2, waiting for transfers between devices, body(): lax.all_to_all(packed, 'lon', split_axis=0, concat_axis=0, tiled=True)  141 us
    gather x2, local copies, waits for them, and re-layouts, body(): jnp.take(target, receivers, axis=0)  20 us
    gather x2, local copies, waits for them, and re-layouts, body(): jnp.take(lookup, senders, axis=0).astype(jnp.float32)  19.3 us
    all_to_all x2, starting transfers between devices, body(): lax.all_to_all(packed, 'lon', split_axis=0, concat_axis=0, tiled=True)  18.5 us
    all_to_all x2, starting transfers between devices, body(): lax.all_to_all(placed, 'lon', split_axis=0, concat_axis=0, tiled=True)  15.3 us
    convert_element_type x2, other arithmetic, body(): jax.nn.silu(summed_terms).astype(jnp.bfloat16)  13 us
    concatenate x2, other arithmetic, extended_2(): x = jnp.concatenate([before, x, after], axis=dim)  9.43 us
    gather x1, local copies, waits for them, and re-layouts, body(): picked = jnp.take(table, inflow_cell.reshape(-1), axis=1)  8.76 us
  transfers between devices with their start and end apart: 16, of which 7 were waited for; matrix products, arithmetic and copies ran while one was open for 43% of the time, Pallas kernels for 0%

commit v1 on v0

v1 whole, which is shorter than its diff:
```python
import jax
import jax.numpy as jnp
from jax import lax
from jax.experimental import pallas as pl
from jax.experimental.pallas import tpu as pltpu
from jax.sharding import PartitionSpec as P

F32, BF16 = jnp.float32, jnp.bfloat16
MESH = pl.DeviceIdType.MESH
MEMBERS = 2
CHANNELS = 192
FEATURES = MEMBERS * CHANNELS
ROWS, COLS = 8, 128
CELLS = ROWS * COLS
BLOCKS, ENTRIES, CAP = 16, 128, 2
NODES = 256
HCAP = 48
EDGES = 1536
HID = 512
LAYERS = 2
N_LAT, N_LON = 8, 16
N_Z = N_LON // 2
GROUP = 48
GROUPS = FEATURES // GROUP
COPIES = 128
VMEM_LIMIT = 66 * 1024 * 1000


def nt_dot(a, b):
    return lax.dot_general(a, b, (((1,), (1,)), ((), ())), preferred_element_type=F32)


def mm(a, b):
    return jnp.dot(a, b, preferred_element_type=F32)


def hot(mask):
    return jnp.where(mask, 1.0, 0.0).astype(BF16)


def silu(v):
    half = 0.5 * v
    return half + half * jnp.tanh(half)


def normalize(values):
    scale = lax.rsqrt(jnp.mean(values * values, axis=-1, keepdims=True) + 1e-06)
    return (values * scale).astype(BF16)


def lanes(shape):
    return lax.broadcasted_iota(jnp.int32, shape, 1)


def sublanes(shape):
    return lax.broadcasted_iota(jnp.int32, shape, 0)


def column(row):
    return jnp.transpose(jnp.broadcast_to(row.astype(F32), (128, 128))).astype(jnp.int32)


def kernel(
    in_source,
    out_source,
    fields_hbm,
    wind_east,
    wind_north,
    diffusion,
    inflow_cell,
    inflow_node,
    inflow_weight,
    encoder_hbm,
    sender_hbm,
    receiver_hbm,
    update_hbm,
    decoder_hbm,
    edge_sender,
    edge_receiver,
    halo_rows,
    outflow_node,
    outflow_cell,
    outflow_weight,
    out_hbm,
    tile,
    state_a,
    state_b,
    lat_out,
    lat_in,
    lon_out,
    lon_in,
    grid_bf,
    cell_hot,
    flow,
    node_hot,
    pack_out,
    pack_in,
    want_in,
    rs_out,
    rs_in,
    rs_y_out,
    rs_y_in,
    rs_last_out,
    rs_last_in,
    node_input,
    edge_hot,
    collect_hot,
    want_hot,
    encoder,
    sender_w,
    receiver_w,
    update_w,
    decoder,
    hidden,
    source_target,
    halo_out,
    halo,
    summed,
    message,
    spread,
    ring,
    ring_y,
    adjust,
    load_sem,
    send_sem,
    recv_sem,
):
    lat = lax.axis_index("lat")
    lon = lax.axis_index("lon")
    z, y = lon // 2, lon % 2
    sides = (
        {"lat": (lat + N_LAT - 1) % N_LAT},
        {"lat": (lat + 1) % N_LAT},
        {"lon": (lon + N_LON - 1) % N_LON},
        {"lon": (lon + 1) % N_LON},
    )
    above = {"lon": (lon + 2) % N_LON}
    below = {"lon": (lon + N_LON - 2) % N_LON}
    partner = {"lon": 2 * z + (1 - y)}
    used = [0]
    started = []

    def copy(src, dst, device):
        index = used[0]
        used[0] += 1
        made = pltpu.make_async_remote_copy(
            src_ref=src,
            dst_ref=dst,
            send_sem=send_sem.at[index],
            recv_sem=recv_sem.at[index],
            device_id=device,
            device_id_type=MESH,
        )
        made.start()
        started.append(made)
        return made

    loads = {}
    for index, (name, src, dst) in enumerate(
        (
            ("fields", fields_hbm, tile),
            ("encoder", encoder_hbm, encoder),
            ("sender", sender_hbm, sender_w),
            ("receiver", receiver_hbm, receiver_w),
            ("update", update_hbm, update_w),
            ("decoder", decoder_hbm, decoder),
        )
    ):
        loads[name] = pltpu.make_async_copy(src, dst, load_sem.at[index])
        loads[name].start()

    barrier = pltpu.get_barrier_semaphore()
    for side in sides[:2]:
        pl.semaphore_signal(barrier, inc=1, device_id=side, device_id_type=MESH)
    for offset in range(1, N_LON):
        pl.semaphore_signal(
            barrier, inc=1, device_id={"lon": (lon + offset) % N_LON}, device_id_type=MESH
        )

    flow[BLOCKS] = jnp.zeros((FEATURES, ENTRIES), BF16)
    for owner in range(N_LON):
        for slot in range(CAP):
            index = out_source[owner * CAP + slot]
            filled = index < BLOCKS
            index = jnp.minimum(index, BLOCKS - 1)
            nodes = outflow_node[pl.ds(index, 1), :].astype(F32)
            pack_out[owner, pl.ds(slot, 1), :] = jnp.where(filled, nodes, -1.0)
            pack_out[owner, pl.ds(2 + slot, 1), :] = outflow_cell[pl.ds(index, 1), :].astype(F32)
            pack_out[owner, pl.ds(4 + slot, 1), :] = outflow_weight[pl.ds(index, 1), :]
        pack_out[owner, pl.ds(6, 2), :] = jnp.zeros((2, ENTRIES), F32)

    loads["fields"].wait()
    for j in range(ROWS):
        state_a[j] = tile[pl.ds(j, FEATURES, stride=ROWS), :]
    pl.semaphore_wait(barrier, N_LON + 1)

    east, north, mix = wind_east[...], wind_north[...], diffusion[...]
    c_west = jnp.maximum(east, 0.0) + mix
    c_east = mix - jnp.minimum(east, 0.0)
    c_south = jnp.maximum(north, 0.0) + mix
    c_north = mix - jnp.minimum(north, 0.0)
    c_middle = 1.0 - jnp.abs(east) - jnp.abs(north) - 4.0 * mix

    lane = lanes((GROUP, COLS))

    def send_edges(state, step):
        lat_out[step, 0] = state[0].astype(BF16)
        lat_out[step, 1] = state[ROWS - 1].astype(BF16)

        def collect(g, carry):
            for j in range(ROWS):
                part = state[j, pl.ds(pl.multiple_of(g * GROUP, GROUP), GROUP), :]
                moved = pltpu.roll(part, 16 * g + 2 * j + 1, 1)
                carry = jnp.where(lane // 2 == 8 * g + j, moved, carry)
            return carry

        edge = lax.fori_loop(0, GROUPS, collect, jnp.zeros((GROUP, COLS), F32))
        lon_out[step] = edge.astype(BF16)
        return [
            copy(lon_out.at[step], lon_in.at[step, 1], sides[2]),
            copy(lon_out.at[step], lon_in.at[step, 0], sides[3]),
            copy(lat_out.at[step, 0], lat_in.at[step, 1], sides[0]),
            copy(lat_out.at[step, 1], lat_in.at[step, 0], sides[1]),
        ]

    def advance(state, result, step, last):
        from_west = pltpu.roll(lon_in[step, 0].astype(F32), 1, 1)
        from_east = pltpu.roll(lon_in[step, 1].astype(F32), COLS - 1, 1)
        joined = jnp.where(lane % 2 == 0, from_east, from_west)

        def group(g, carry):
            at = pl.ds(pl.multiple_of(g * GROUP, GROUP), GROUP)
            low = jnp.where(lat == 0, state[0, at, :], lat_in[step, 0, at, :].astype(F32))
            high = jnp.where(
                lat == N_LAT - 1, state[ROWS - 1, at, :], lat_in[step, 1, at, :].astype(F32)
            )
            for j in range(ROWS):
                m = state[j, at, :]
                s = low if j == 0 else state[j - 1, at, :]
                n = high if j == ROWS - 1 else state[j + 1, at, :]
                ends = pltpu.roll(joined, 2 * COLS - (16 * g + 2 * j + 1), 1)
                w = jnp.where(lane == 0, ends, pltpu.roll(m, 1, 1))
                e = jnp.where(lane == COLS - 1, ends, pltpu.roll(m, COLS - 1, 1))
                row = slice(j, j + 1)
                value = m * c_middle[row] + w * c_west[row] + e * c_east[row]
                value = value + s * c_south[row] + n * c_north[row]
                result[j, at, :] = value
                if last:
                    grid_bf[at, j * COLS : (j + 1) * COLS] = value.astype(BF16)
            return carry

        lax.fori_loop(0, GROUPS, group, 0)

    first_edges = send_edges(state_a, 0)
    wanted = [
        copy(halo_rows, want_in.at[1], sides[0]),
        copy(halo_rows, want_in.at[0], sides[1]),
        copy(halo_rows, want_in.at[3], sides[2]),
        copy(halo_rows, want_in.at[2], sides[3]),
    ]
    packs = []
    for offset in range(1, N_LON):
        other = (lon + offset) % N_LON
        packs.append(copy(pack_out.at[other], pack_in.at[offset], {"lon": other}))
    pack_in[0] = pack_out[lon]

    def cell_table(k, carry):
        for half in range(2):
            cells = inflow_cell[pl.ds(2 * k + half, 1), :]
            for j in range(ROWS):
                cell_hot[k, j * COLS : (j + 1) * COLS, half * 128 : (half + 1) * 128] = hot(
                    sublanes((COLS, ENTRIES)) + j * COLS == cells
                )
        return carry

    lax.fori_loop(0, BLOCKS // 2, cell_table, 0)
    for c in first_edges:
        c.wait_recv()
    advance(state_a, state_b, 0, False)
    second_edges = send_edges(state_b, 1)

    def node_table(r, carry):
        node_hot[r] = hot(sublanes((NODES, ENTRIES)) == inflow_node[pl.ds(r, 1), :])
        return carry

    lax.fori_loop(0, BLOCKS, node_table, 0)
    node_hot[BLOCKS] = jnp.zeros((NODES, ENTRIES), BF16)
    for c in second_edges:
        c.wait_recv()
    advance(state_b, state_a, 1, True)

    def gather(k, carry):
        picked = mm(grid_bf[...], cell_hot[k])
        flow[2 * k] = (picked[:, :ENTRIES] * inflow_weight[pl.ds(2 * k, 1), :]).astype(BF16)
        flow[2 * k + 1] = (picked[:, ENTRIES:] * inflow_weight[pl.ds(2 * k + 1, 1), :]).astype(BF16)
        return carry

    lax.fori_loop(0, BLOCKS // 2, gather, 0)

    def share(dz, other, member):
        owner = 2 * ((z + dz + N_Z) % N_Z) + (1 - y if other else y)
        first, second = in_source[owner * CAP], in_source[owner * CAP + 1]
        rows = pl.ds(member * CHANNELS, CHANNELS)
        values = jnp.concatenate([flow[first, rows, :], flow[second, rows, :]], axis=1)
        places = jnp.concatenate([node_hot[first], node_hot[second]], axis=1)
        return nt_dot(values, places)

    order = (4, -3, 3, -2, 2, -1, 1, 0)
    hops = ((4, 3), (3, 4), (4, 3))
    y_copies, chains = {}, {}

    def send_y(k):
        rs_y_out[k] = share(order[k], True, 1).astype(BF16)
        y_copies[k] = copy(rs_y_out.at[k], rs_y_in.at[k], partner)

    def part(stream, dz):
        if stream < 2:
            return share(dz, stream == 0, 0)
        k = order.index(dz)
        y_copies[k].wait_recv()
        return share(dz, False, 1) + rs_y_in[k].astype(F32)

    def step_z(stream, s):
        for way in range(2):
            length = hops[stream][way]
            if s >= length:
                continue
            dz = (length - s) * (1 if way == 0 else -1)
            value = part(stream, dz)
            if s:
                chains[stream, way, s - 1].wait_recv()
                value = value + rs_in[stream, way, s - 1].astype(F32)
            rs_out[stream, way, s] = value.astype(BF16)
            chains[stream, way, s] = copy(
                rs_out.at[stream, way, s],
                rs_in.at[stream, way, s],
                above if way == 0 else below,
            )

    def end_z(stream):
        value = part(stream, 0)
        for way in range(2):
            last = hops[stream][way] - 1
            chains[stream, way, last].wait_recv()
            value = value + rs_in[stream, way, last].astype(F32)
        return value

    send_y(0)
    send_y(1)
    step_z(0, 0)
    step_z(1, 0)
    for k in range(2, 8):
        send_y(k)
    step_z(2, 0)

    def edge_table(k, carry):
        at = pl.ds(pl.multiple_of(k * 128, 128), 128)
        senders, receivers = edge_sender[pl.ds(k, 1), :], edge_receiver[pl.ds(k, 1), :]
        from_column, to_column = column(senders), column(receivers)
        for part_of in range(2):
            spot = lanes((128, 128)) + part_of * 128
            columns = slice(part_of * 128, part_of * 128 + 128)
            edge_hot[at, columns] = hot(from_column == spot)
            edge_hot[at, 256 + part_of * 128 : 384 + part_of * 128] = hot(to_column == spot)
            edge_hot[at, 512 + part_of * 128 : 640 + part_of * 128] = hot(
                from_column == spot + NODES
            )
            collect_hot[columns, at] = hot(sublanes((128, 128)) + part_of * 128 == receivers)
        return carry

    lax.fori_loop(0, EDGES // 128, edge_table, 0)
    for c in wanted:
        c.wait_recv()
    for q in range(4):
        rows = column(want_in[q, (q ^ 1) : (q ^ 1) + 1, :])[:HCAP]
        for part_of in range(2):
            want_hot[q, :, part_of * 128 : part_of * 128 + 128] = hot(
                rows == lanes((HCAP, 128)) + part_of * 128
            )
    for layer in range(LAYERS):
        halo[layer * NODES + 4 * HCAP : (layer + 1) * NODES, :] = jnp.zeros(
            (NODES - 4 * HCAP, MEMBERS * HID), BF16
        )

    for stream in range(3):
        step_z(stream, 1)
    for c in packs:
        c.wait_recv()

    def spread_table(k, carry):
        rows = pack_in[k]
        spot = sublanes((NODES, ENTRIES)).astype(F32)
        weights, places = [], []
        for slot in range(CAP):
            weights.append(
                jnp.where(spot == rows[slot : slot + 1], rows[4 + slot : 5 + slot], 0.0).astype(BF16)
            )
        weighted = jnp.concatenate(weights, axis=1)
        for j in range(4):
            places = [
                hot(spot + j * NODES == rows[2 + slot : 3 + slot]) for slot in range(CAP)
            ]
            spread[k, :, j * NODES : (j + 1) * NODES] = nt_dot(
                weighted, jnp.concatenate(places, axis=1)
            ).astype(BF16)
        return carry

    lax.fori_loop(0, 8, spread_table, 0)
    for stream in range(3):
        step_z(stream, 2)
    lax.fori_loop(8, 16, spread_table, 0)
    for stream in range(3):
        step_z(stream, 3)
    rs_last_out[...] = end_z(0).astype(BF16)
    last_y = copy(rs_last_out, rs_last_in, partner)
    near = end_z(1)
    node_input[CHANNELS:, :] = end_z(2)
    last_y.wait_recv()
    node_input[:CHANNELS, :] = near + rs_last_in[...].astype(F32)

    for name in ("encoder", "sender", "receiver", "update", "decoder"):
        loads[name].wait()
    turned = jnp.transpose(node_input[...]).astype(BF16)
    for m in range(MEMBERS):
        rows = pl.ds(m * NODES, NODES)
        hidden[rows, :] = silu(mm(turned[:, m * CHANNELS : (m + 1) * CHANNELS], encoder[...]))

    for layer in range(LAYERS):
        normed = normalize(hidden[...])
        source = mm(normed, sender_w[layer]).astype(BF16)
        source_target[:NODES, :HID] = source[:NODES]
        source_target[:NODES, HID:] = source[NODES:]
        travelling = []
        for q in range(4):
            halo_out[layer, q] = mm(want_hot[q], source_target[:NODES, :]).astype(BF16)
        for q in (2, 3, 0, 1):
            travelling.append(
                copy(halo_out.at[layer, q], halo_slot(halo, layer, q ^ 1), sides[q])
            )
        target = mm(normed, receiver_w[layer]).astype(BF16)
        source_target[NODES:, :HID] = target[:NODES]
        source_target[NODES:, HID:] = target[NODES:]

        def near_part(k, carry):
            at = pl.ds(pl.multiple_of(k * 256, 256), 256)
            summed[at, :] = mm(edge_hot[at, : 2 * NODES], source_target[...])
            return carry

        lax.fori_loop(0, EDGES // 256, near_part, 0)
        for c in travelling:
            c.wait_recv()
        base = layer * NODES

        def far_part(k, carry):
            at = pl.ds(pl.multiple_of(k * 256, 256), 256)
            value = summed[at, :] + mm(
                edge_hot[at, 2 * NODES :], halo[pl.ds(base, NODES), :]
            )
            message[at, :] = silu(value).astype(BF16)
            return carry

        lax.fori_loop(0, EDGES // 256, far_part, 0)
        collected = mm(collect_hot[...], message[...]).astype(BF16)
        for m in range(MEMBERS):
            rows = pl.ds(m * NODES, NODES)
            hidden[rows, :] += mm(collected[:, m * HID : (m + 1) * HID], update_w[layer])

    final = normalize(hidden[...])
    ring[0, 0] = nt_dot(decoder[...], final[:NODES]).astype(BF16)
    ring[2, 0] = nt_dot(decoder[...], final[NODES:]).astype(BF16)
    across = copy(ring.at[0, 0], ring.at[1, 0], partner)
    lengths = ((3, 4), (4, 3), (4, 3))
    moves, y_moves = {}, {}

    def slot_of(way, s):
        return s if way == 0 else (N_Z - s) % N_Z

    def forward(stream, s):
        for way in range(2):
            if s and s <= lengths[stream][way]:
                moves[stream, way, s - 1].wait_recv()
                if stream == 2:
                    here = slot_of(way, s)
                    y_moves[here] = copy(ring.at[2, here], ring_y.at[here], partner)
            if s < lengths[stream][way]:
                moves[stream, way, s] = copy(
                    ring.at[stream, slot_of(way, s)],
                    ring.at[stream, slot_of(way, s + 1)],
                    above if way == 0 else below,
                )

    def add(stream, slots, member):
        total = None
        for here in slots:
            if stream in (0, 2):
                k = (2 * here) % N_LON
            else:
                k = (2 * here + 2 * y + N_LON - 1) % N_LON
            values = ring_y[here] if stream == 3 else ring[stream, here]
            term = mm(values, spread[k])
            total = term if total is None else total + term
        adjust[member] += total

    def arrived(stream, s):
        if s == 0:
            return [0]
        return [slot_of(way, s) for way in range(2) if s <= lengths[stream][way]]

    forward(2, 0)
    forward(0, 0)
    y_moves[0] = copy(ring.at[2, 0], ring_y.at[0], partner)
    for m in range(MEMBERS):
        for j in range(ROWS):
            adjust[m, :, j * COLS : (j + 1) * COLS] = state_a[
                j, m * CHANNELS : (m + 1) * CHANNELS, :
            ]
    add(0, [0], 0)
    add(2, [0], 1)
    across.wait_recv()
    forward(1, 0)
    for s in range(1, 5):
        for stream in (2, 0, 1):
            forward(stream, s)
        add(1, arrived(1, s - 1), 0)
        for here in arrived(2, s - 1):
            y_moves[here].wait_recv()
        add(3, arrived(2, s - 1), 1)
        add(2, arrived(2, s), 1)
        add(0, arrived(0, s), 0)
    add(1, arrived(1, 4), 0)
    for here in arrived(2, 4):
        y_moves[here].wait_recv()
    add(3, arrived(2, 4), 1)

    for m in range(MEMBERS):
        for j in range(ROWS):
            tile[pl.ds(m * CHANNELS * ROWS + j, CHANNELS, stride=ROWS), :] = adjust[
                m, :, j * COLS : (j + 1) * COLS
            ]
    done = pltpu.make_async_copy(tile, out_hbm, load_sem.at[6])
    done.start()
    for c in started:
        c.wait_send()
    done.wait()


def halo_slot(halo, layer, q):
    return halo.at[pl.ds(layer * NODES + q * HCAP, HCAP), :]


def blocks_of(owners):
    owner = owners[:, 0]
    same = (owner[:, None] == owner[None, :]).astype(jnp.int32)
    earlier = jnp.sum(jnp.tril(same, -1), axis=1)
    slot = owner * CAP + earlier
    hits = slot[None, :] == jnp.arange(N_LON * CAP, dtype=jnp.int32)[:, None]
    return jnp.min(jnp.where(hits, jnp.arange(BLOCKS, dtype=jnp.int32)[None, :], BLOCKS), axis=1)


def body(
    fields,
    wind_east,
    wind_north,
    diffusion,
    inflow_owner,
    inflow_cell,
    inflow_node,
    inflow_weight,
    encoder,
    sender_weight,
    receiver_weight,
    update_weight,
    decoder,
    edge_sender,
    edge_receiver,
    halo_rows,
    outflow_owner,
    outflow_node,
    outflow_cell,
    outflow_weight,
):
    vmem = pl.BlockSpec(memory_space=pltpu.VMEM)
    smem = pl.BlockSpec(memory_space=pltpu.SMEM)
    anywhere = pl.BlockSpec(memory_space=pl.ANY)
    wanted = jnp.pad(halo_rows.reshape(4, HCAP), ((0, 4), (0, 128 - HCAP)))
    half = (CHANNELS, NODES)
    scratch = [
        pltpu.VMEM((FEATURES * ROWS, COLS), F32),
        pltpu.VMEM((ROWS, FEATURES, COLS), F32),
        pltpu.VMEM((ROWS, FEATURES, COLS), F32),
        pltpu.VMEM((2, 2, FEATURES, COLS), BF16),
        pltpu.VMEM((2, 2, FEATURES, COLS), BF16),
        pltpu.VMEM((2, GROUP, COLS), BF16),
        pltpu.VMEM((2, 2, GROUP, COLS), BF16),
        pltpu.VMEM((FEATURES, CELLS), BF16),
        pltpu.VMEM((BLOCKS // 2, CELLS, 2 * ENTRIES), BF16),
        pltpu.VMEM((BLOCKS + 1, FEATURES, ENTRIES), BF16),
        pltpu.VMEM((BLOCKS + 1, NODES, ENTRIES), BF16),
        pltpu.VMEM((N_LON, 8, ENTRIES), F32),
        pltpu.VMEM((N_LON, 8, ENTRIES), F32),
        pltpu.VMEM((4, 8, 128), jnp.int32),
        pltpu.VMEM((3, 2, 4) + half, BF16),
        pltpu.VMEM((3, 2, 4) + half, BF16),
        pltpu.VMEM((N_Z,) + half, BF16),
        pltpu.VMEM((N_Z,) + half, BF16),
        pltpu.VMEM(half, BF16),
        pltpu.VMEM(half, BF16),
        pltpu.VMEM((FEATURES, NODES), F32),
        pltpu.VMEM((EDGES, 3 * NODES), BF16),
        pltpu.VMEM((NODES, EDGES), BF16),
        pltpu.VMEM((4, HCAP, NODES), BF16),
        pltpu.VMEM((CHANNELS, HID), BF16),
        pltpu.VMEM((LAYERS, HID, HID), BF16),
        pltpu.VMEM((LAYERS, HID, HID), BF16),
        pltpu.VMEM((LAYERS, HID, HID), BF16),
        pltpu.VMEM((CHANNELS, HID), BF16),
        pltpu.VMEM((MEMBERS * NODES, HID), F32),
        pltpu.VMEM((2 * NODES, MEMBERS * HID), BF16),
        pltpu.VMEM((LAYERS, 4, HCAP, MEMBERS * HID), BF16),
        pltpu.VMEM((LAYERS * NODES, MEMBERS * HID), BF16),
        pltpu.VMEM((EDGES, MEMBERS * HID), F32),
        pltpu.VMEM((EDGES, MEMBERS * HID), BF16),
        pltpu.VMEM((N_LON, NODES, CELLS), BF16),
        pltpu.VMEM((3, N_Z) + half, BF16),
        pltpu.VMEM((N_Z,) + half, BF16),
        pltpu.VMEM((MEMBERS, CHANNELS, CELLS), F32),
        pltpu.SemaphoreType.DMA((8,)),
        pltpu.SemaphoreType.DMA((COPIES,)),
        pltpu.SemaphoreType.DMA((COPIES,)),
    ]
    result = pl.pallas_call(
        kernel,
        out_shape=jax.ShapeDtypeStruct((FEATURES * ROWS, COLS), F32),
        in_specs=[smem, smem, anywhere]
        + [vmem] * 6
        + [anywhere] * 5
        + [vmem] * 6,
        out_specs=anywhere,
        scratch_shapes=scratch,
        compiler_params=pltpu.CompilerParams(
            collective_id=0, has_side_effects=True, vmem_limit_bytes=VMEM_LIMIT
        ),
    )(
        blocks_of(inflow_owner),
        blocks_of(outflow_owner),
        fields.reshape(FEATURES * ROWS, COLS),
        wind_east,
        wind_north,
        diffusion,
        inflow_cell,
        inflow_node,
        inflow_weight,
        encoder,
        sender_weight,
        receiver_weight,
        update_weight,
        decoder.T,
        edge_sender.reshape(EDGES // 128, 128),
        edge_receiver.reshape(EDGES // 128, 128),
        wanted,
        outflow_node,
        outflow_cell,
        outflow_weight,
    )
    return result.reshape(MEMBERS, CHANNELS, ROWS, COLS)


def solution(mesh):
    placed = (
        P("member", None, "lat", "lon"),
        P("lat", "lon"),
        P("lat", "lon"),
        P("lat", "lon"),
        P(("lat", "lon"), None),
        P(("lat", "lon"), None),
        P(("lat", "lon"), None),
        P(("lat", "lon"), None),
        P(),
        P(),
        P(),
        P(),
        P(),
        P("lat", "lon", None),
        P("lat", "lon", None),
        P("lat", "lon", None, None),
        P(("lat", "lon"), None),
        P(("lat", "lon"), None),
        P(("lat", "lon"), None),
        P(("lat", "lon"), None),
    )
    return jax.shard_map(
        body, mesh=mesh, in_specs=placed, out_specs=P("member", None, "lat", "lon"), check_vma=False
    )
```

time: 394 us -> 123 us (0.31); the launches traced: 388 us -> 123 us
  waiting for transfers between devices: 150 us -> 0 us
  Pallas kernels: 0 us -> 113 us
  local copies, waits for them, and re-layouts: 106 us -> 3.93 us
  starting transfers between devices: 56.5 us -> 0 us
  other arithmetic: 57 us -> 5.49 us
  matrix products: 17.3 us -> 0 us
    all_to_all x4 -> x0, waiting for transfers between devices: 141 us -> none  [the longest x2 141 us: body(): lax.all_to_all(packed, 'lon', split_axis=0, concat_axis=0, tiled=True)]
    pallas_call x0 -> x1, Pallas kernels: none -> 113 us  [body(): pl.pallas_call(kernel, out_shape=jax.ShapeDtypeStruct((FEATURES * ROWS, C...]
    gather x18 -> x0, local copies, waits for them, and re-layouts: 77 us -> none  [the longest x2 20 us: body(): jnp.take(target, receivers, axis=0)]
    all_to_all x4 -> x0, starting transfers between devices: 33.8 us -> none  [the longest x2 18.5 us: body(): lax.all_to_all(packed, 'lon', split_axis=0, concat_axis=0, tiled=True)]
    ppermute x12 -> x0, starting transfers between devices: 22.7 us -> none  [the longest x4 8.71 us: with_halo(): lax.ppermute(first, axis, [(b, a) for a, b in up])]
    dot_general x12 -> x0, matrix products: 17.3 us -> none  [the longest x2 6.1 us: body(): jnp.dot(gather_table, message, preferred_element_type=jnp.float32)]
    convert_element_type x6 -> x0, other arithmetic: 16.5 us -> none  [the longest x2 13 us: body(): jax.nn.silu(summed_terms).astype(jnp.bfloat16)]
    select_n x12 -> x0, other arithmetic: 15.6 us -> none  [the longest x2 8.12 us: place_blocks(): jnp.where(filled[:, None, None], jnp.take(values, source_block, axis=0),...]
  transfers between devices with their start and end apart: 16 -> 0, of which waited for: 7 -> 0; matrix products, arithmetic and copies ran while one was open for 43% -> 0% of each run, Pallas kernels for 0% -> 0%
where the time goes in v1:
time: 123 us
  Pallas kernels  113 us (92%)
  other arithmetic  5.49 us (4%)
  local copies, waits for them, and re-layouts  3.93 us (3%)
    pallas_call x1, Pallas kernels, body(): pl.pallas_call(kernel, out_shape=jax.ShapeDtypeStruct((FEATURES * ROWS, C...  113 us
    unnamed x1, local copies, waits for them, and re-layouts  2.65 us
    unnamed x2, other arithmetic  2.61 us

profile of v1, /device:TPU:2, one launch (start us, length us, event | category | flops | bytes accessed | tf_op | source)
XLA Modules:
  0.0 122.7 jit_solution(8225277453969780438)
XLA Ops:
  0.0 0.9 select_reduce_fusion.1
  0.9 0.7 multiply_add_fusion
  1.6 0.7 select_reduce_fusion.out_source
  2.3 0.6 select_reduce_fusion.2.in_source
  2.9 1.3 %pad.4.halo_rows = s32[8,128]{1,0:T(8,128)} pad(s32[4,48]{1,0:T(4,128)} %bitcast.17, s32[]{:T(128)} %constant.12.clone.1), padding=0_4x0_80 | pad | bytes 4868 | tf_op jit(solution)/shard_map/jit(_pad)/pad | solution.py:585
  4.2 1.3 %reduce = s32[1536]{0:T(1024)} reduce(s32[1,1,1536]{2,1,0:T(1,128)} %param.33, s32[]{:T(128)} %constant.12.clone.1), dimensions={0,1}, to_apply=%param.33.reduce_sub_computation | reduce | bytes 12292 | tf_op args[13]
  5.5 1.3 %reduce.1 = s32[1536]{0:T(1024)} reduce(s32[1,1,1536]{2,1,0:T(1,128)} %param.34, s32[]{:T(128)} %constant.12.clone.1), dimensions={0,1}, to_apply=%param.34.reduce_sub_computation | reduce | bytes 12292 | tf_op args[14]
  6.8 113.2 %shard_map.190 = f32[3072,128]{1,0:T(8,128)} custom-call(s32[32]{0:T(128)} %select_reduce_fusion.2.in_source, s32[32]{0:T(128)} %select_reduce_fusion.out_source, f32[3072,128]{1,0:T(8,128)} %bitcast.11, f32[8,128]{1,0:T(8,128)} %wind_east.1, f32[8,128]{1,0:T(8,128)} %wind_north.1, f32[8,128]{1,0:T(8,128)} %diffusion.1, s32[16,128]{1,0:T(8,128)} %inflow_cell.1, ...), custom_call_target="tpu_custom_call" | custom-call | tf_op jit(solution)/shard_map/pallas_call | solution.py:631
  120.0 2.7 %copy.22 = f32[2,192,8,128]{3,2,1,0:T(8,128)} copy(f32[2,192,8,128]{3,2,1,0:T(8,128)} %bitcast.10) | data formatting | bytes 3145728
  (1 shorter events, 0.0 us)

commit v2 on v1

v2 whole, which is shorter than its diff:
```python
import jax
import jax.numpy as jnp
from jax import lax
from jax.experimental import pallas as pl
from jax.experimental.pallas import tpu as pltpu
from jax.sharding import PartitionSpec as P

F32, BF16 = jnp.float32, jnp.bfloat16
MESH = pl.DeviceIdType.MESH
MEMBERS = 2
CHANNELS = 192
FEATURES = MEMBERS * CHANNELS
ROWS, COLS = 8, 128
CELLS = ROWS * COLS
BLOCKS, ENTRIES, CAP = 16, 128, 2
NODES = 256
HCAP = 48
EDGES = 1536
HID = 512
LAYERS = 2
DSTEPS = 2
N_LAT, N_LON = 8, 16
N_Z = N_LON // 2
GROUP = 48
GROUPS = CHANNELS // GROUP
HALF = CHANNELS // 2
COPIES = 192
VMEM_LIMIT = 63 * 1024 * 1024


def nt_dot(a, b):
    return lax.dot_general(a, b, (((1,), (1,)), ((), ())), preferred_element_type=F32)


def mm(a, b):
    return jnp.dot(a, b, preferred_element_type=F32)


def hot(mask):
    return jnp.where(mask, 1.0, 0.0).astype(BF16)


def silu(v):
    half = 0.5 * v
    return half + half * jnp.tanh(half)


def normalize(values):
    scale = lax.rsqrt(jnp.mean(values * values, axis=-1, keepdims=True) + 1e-06)
    return (values * scale).astype(BF16)


def lanes(shape):
    return lax.broadcasted_iota(jnp.int32, shape, 1)


def sublanes(shape):
    return lax.broadcasted_iota(jnp.int32, shape, 0)


def column(row):
    return jnp.transpose(jnp.broadcast_to(row.astype(F32), (128, 128))).astype(jnp.int32)


def kernel(
    inflow_owner,
    outflow_owner,
    fields_hbm,
    wind_east,
    wind_north,
    diffusion,
    inflow_cell,
    inflow_node,
    inflow_weight,
    encoder_hbm,
    sender_hbm,
    receiver_hbm,
    update_hbm,
    decoder_hbm,
    edge_sender,
    edge_receiver,
    halo_rows,
    outflow_node,
    outflow_cell,
    outflow_weight,
    out_hbm,
    tile,
    state_a,
    state_b,
    lat_out,
    lat_in,
    lon_out,
    lon_in,
    grid_bf,
    cell_hot,
    flow,
    node_hot,
    pack_out,
    pack_in,
    want_in,
    shares,
    rs_out,
    rs_in,
    rs_y_out,
    rs_y_in,
    rs_last_out,
    rs_last_in,
    node_input,
    edge_hot,
    collect_hot,
    want_hot,
    encoder,
    sender_w,
    receiver_w,
    update_w,
    decoder,
    hidden,
    source_target,
    halo_out,
    halo,
    summed,
    message,
    spread,
    both,
    adjust,
    in_source,
    want_out,
    load_sem,
    send_sem,
    recv_sem,
):
    lat = lax.axis_index("lat")
    lon = lax.axis_index("lon")
    z, y = lon // 2, lon % 2
    sides = (
        {"lat": (lat + N_LAT - 1) % N_LAT},
        {"lat": (lat + 1) % N_LAT},
        {"lon": (lon + N_LON - 1) % N_LON},
        {"lon": (lon + 1) % N_LON},
    )
    above = {"lon": (lon + 2) % N_LON}
    below = {"lon": (lon + N_LON - 2) % N_LON}
    partner = {"lon": 2 * z + (1 - y)}
    used = [0]
    started = []

    def copy(src, dst, device):
        index = used[0]
        used[0] += 1
        made = pltpu.make_async_remote_copy(
            src_ref=src,
            dst_ref=dst,
            send_sem=send_sem.at[index],
            recv_sem=recv_sem.at[index],
            device_id=device,
            device_id_type=MESH,
        )
        made.start()
        started.append(made)
        return made

    loads = {}
    for index, (name, src, dst) in enumerate(
        (
            ("fields0", fields_hbm.at[0], tile.at[0]),
            ("fields1", fields_hbm.at[1], tile.at[1]),
            ("encoder", encoder_hbm, encoder),
            ("sender", sender_hbm, sender_w),
            ("receiver", receiver_hbm, receiver_w),
            ("update", update_hbm, update_w),
            ("decoder", decoder_hbm, decoder),
        )
    ):
        loads[name] = pltpu.make_async_copy(src, dst, load_sem.at[index])
        loads[name].start()

    barrier = pltpu.get_barrier_semaphore()
    for side in sides[:2]:
        pl.semaphore_signal(barrier, inc=1, device_id=side, device_id_type=MESH)
    for offset in range(1, N_LON):
        pl.semaphore_signal(
            barrier, inc=1, device_id={"lon": (lon + offset) % N_LON}, device_id_type=MESH
        )

    def blocks_of(owners, owner):
        first, second = jnp.int32(BLOCKS), jnp.int32(BLOCKS)
        for r in reversed(range(BLOCKS)):
            same = owners[0, r] == owner
            second = jnp.where(same, first, second)
            first = jnp.where(same, r, first)
        return first, second

    for owner in range(N_LON):
        pair = blocks_of(inflow_owner, owner)
        for slot in range(CAP):
            in_source[owner * CAP + slot] = pair[slot]
    want_out[...] = jnp.zeros((8, 128), jnp.int32)
    want_out[:4, :HCAP] = halo_rows[0, 0]

    flow[BLOCKS] = jnp.zeros((FEATURES, ENTRIES), BF16)
    for owner in range(N_LON):
        pair = blocks_of(outflow_owner, owner)
        for slot in range(CAP):
            index = pair[slot]
            filled = index < BLOCKS
            index = jnp.minimum(index, BLOCKS - 1)
            nodes = outflow_node[pl.ds(index, 1), :].astype(F32)
            pack_out[owner, pl.ds(slot, 1), :] = jnp.where(filled, nodes, -1.0)
            pack_out[owner, pl.ds(2 + slot, 1), :] = outflow_cell[pl.ds(index, 1), :].astype(F32)
            pack_out[owner, pl.ds(4 + slot, 1), :] = outflow_weight[pl.ds(index, 1), :]
        pack_out[owner, pl.ds(6, 2), :] = jnp.zeros((2, ENTRIES), F32)

    for m in range(MEMBERS):
        loads[f"fields{m}"].wait()
        for j in range(ROWS):
            state_a[j, m * CHANNELS : (m + 1) * CHANNELS, :] = tile[
                m, pl.ds(j, CHANNELS, stride=ROWS), :
            ]
    pl.semaphore_wait(barrier, N_LON + 1)

    east, north, mix = wind_east[...], wind_north[...], diffusion[...]
    c_west = jnp.maximum(east, 0.0) + mix
    c_east = mix - jnp.minimum(east, 0.0)
    c_south = jnp.maximum(north, 0.0) + mix
    c_north = mix - jnp.minimum(north, 0.0)
    c_middle = 1.0 - jnp.abs(east) - jnp.abs(north) - 4.0 * mix

    lane = lanes((GROUP, COLS))

    def send_edges(state, step, m):
        rows = slice(m * CHANNELS, (m + 1) * CHANNELS)
        lat_out[step, m, 0] = state[0, rows].astype(BF16)
        lat_out[step, m, 1] = state[ROWS - 1, rows].astype(BF16)

        def collect(g, carry):
            at = pl.ds(pl.multiple_of(m * CHANNELS + g * GROUP, GROUP), GROUP)
            for j in range(ROWS):
                moved = pltpu.roll(state[j, at, :], 16 * g + 2 * j + 1, 1)
                carry = jnp.where(lane // 2 == 8 * g + j, moved, carry)
            return carry

        edge = lax.fori_loop(0, GROUPS, collect, jnp.zeros((GROUP, COLS), F32))
        lon_out[step, m] = edge.astype(BF16)
        return [
            copy(lon_out.at[step, m], lon_in.at[step, m, 1], sides[2]),
            copy(lon_out.at[step, m], lon_in.at[step, m, 0], sides[3]),
            copy(lat_out.at[step, m, 0], lat_in.at[step, m, 1], sides[0]),
            copy(lat_out.at[step, m, 1], lat_in.at[step, m, 0], sides[1]),
        ]

    def advance(state, result, step, m, last):
        from_west = pltpu.roll(lon_in[step, m, 0].astype(F32), 1, 1)
        from_east = pltpu.roll(lon_in[step, m, 1].astype(F32), COLS - 1, 1)
        joined = jnp.where(lane % 2 == 0, from_east, from_west)

        def group(g, carry):
            inner = pl.ds(pl.multiple_of(g * GROUP, GROUP), GROUP)
            at = pl.ds(pl.multiple_of(m * CHANNELS + g * GROUP, GROUP), GROUP)
            low = jnp.where(lat == 0, state[0, at, :], lat_in[step, m, 0, inner, :].astype(F32))
            high = jnp.where(
                lat == N_LAT - 1,
                state[ROWS - 1, at, :],
                lat_in[step, m, 1, inner, :].astype(F32),
            )
            for j in range(ROWS):
                center = state[j, at, :]
                s = low if j == 0 else state[j - 1, at, :]
                n = high if j == ROWS - 1 else state[j + 1, at, :]
                ends = pltpu.roll(joined, 2 * COLS - (16 * g + 2 * j + 1), 1)
                w = jnp.where(lane == 0, ends, pltpu.roll(center, 1, 1))
                e = jnp.where(lane == COLS - 1, ends, pltpu.roll(center, COLS - 1, 1))
                row = slice(j, j + 1)
                value = center * c_middle[row] + w * c_west[row] + e * c_east[row]
                value = value + s * c_south[row] + n * c_north[row]
                result[j, at, :] = value
                if last:
                    grid_bf[at, j * COLS : (j + 1) * COLS] = value.astype(BF16)
            return carry

        lax.fori_loop(0, GROUPS, group, 0)

    def arrive(copies):
        for c in copies:
            c.wait_recv()

    first = [send_edges(state_a, 0, m) for m in range(MEMBERS)]
    wanted = [
        copy(want_out, want_in.at[1], sides[0]),
        copy(want_out, want_in.at[0], sides[1]),
        copy(want_out, want_in.at[3], sides[2]),
        copy(want_out, want_in.at[2], sides[3]),
    ]
    packs = []
    for offset in range(1, N_LON):
        other = (lon + offset) % N_LON
        packs.append(copy(pack_out.at[other], pack_in.at[offset], {"lon": other}))
    pack_in[0] = pack_out[lon]

    def cell_table(k, carry):
        for half in range(2):
            cells = inflow_cell[pl.ds(2 * k + half, 1), :]
            for j in range(ROWS):
                cell_hot[k, j * COLS : (j + 1) * COLS, half * 128 : (half + 1) * 128] = hot(
                    sublanes((COLS, ENTRIES)) + j * COLS == cells
                )
        return carry

    lax.fori_loop(0, BLOCKS // 2, cell_table, 0)
    def edge_table(k, carry):
        at = pl.ds(pl.multiple_of(k * 128, 128), 128)
        senders, receivers = edge_sender[0, :, at], edge_receiver[0, :, at]
        from_column, to_column = column(senders), column(receivers)
        for part_of in range(2):
            spot = lanes((128, 128)) + part_of * 128
            columns = slice(part_of * 128, part_of * 128 + 128)
            edge_hot[at, columns] = hot(from_column == spot)
            edge_hot[at, 256 + part_of * 128 : 384 + part_of * 128] = hot(to_column == spot)
            edge_hot[at, 512 + part_of * 128 : 640 + part_of * 128] = hot(
                from_column == spot + NODES
            )
            collect_hot[columns, at] = hot(sublanes((128, 128)) + part_of * 128 == receivers)
        return carry

    lax.fori_loop(0, EDGES // 128, edge_table, 0)
    second = []
    for m in range(MEMBERS):
        arrive(first[m])
        advance(state_a, state_b, 0, m, False)
        second.append(send_edges(state_b, 1, m))

    def node_table(r, carry):
        node_hot[r] = hot(sublanes((NODES, ENTRIES)) == inflow_node[pl.ds(r, 1), :])
        return carry

    lax.fori_loop(0, BLOCKS, node_table, 0)
    node_hot[BLOCKS] = jnp.zeros((NODES, ENTRIES), BF16)

    def gather(k, carry):
        picked = mm(grid_bf[...], cell_hot[k])
        for half in range(2):
            weights = inflow_weight[pl.ds(2 * k + half, 1), :]
            flow[2 * k + half] = (
                picked[:, half * ENTRIES : (half + 1) * ENTRIES] * weights
            ).astype(BF16)
        return carry

    known = set()

    def share(m, dz, other, rows):
        spot = 2 * (dz % N_Z) + (1 if other else 0)
        if spot not in known:
            known.add(spot)
            owner = 2 * ((z + dz + N_Z) % N_Z) + (1 - y if other else y)
            one, two = in_source[owner * CAP], in_source[owner * CAP + 1]
            values = jnp.concatenate([flow[one], flow[two]], axis=1)
            places = jnp.concatenate([node_hot[one], node_hot[two]], axis=1)
            shares[spot] = nt_dot(values, places)
        return shares[spot, m * CHANNELS + rows.start : m * CHANNELS + rows.stop]

    order = (4, -3, 3, -2, 2, -1, 1, 0)
    hops = ((4, 3), (3, 4), (4, 3))
    lower, upper = slice(0, HALF), slice(HALF, CHANNELS)

    def reduce_scatter(m):
        y_copies, chains = {}, {}

        def send_y(k):
            rs_y_out[m, k] = share(m, order[k], True, upper).astype(BF16)
            y_copies[k] = copy(rs_y_out.at[m, k], rs_y_in.at[m, k], partner)

        def part(stream, dz):
            if stream < 2:
                return share(m, dz, stream == 0, lower)
            k = order.index(dz)
            y_copies[k].wait_recv()
            return share(m, dz, False, upper) + rs_y_in[m, k].astype(F32)

        def step_z(stream, s):
            for way in range(2):
                length = hops[stream][way]
                if s >= length:
                    continue
                dz = (length - s) * (1 if way == 0 else -1)
                value = part(stream, dz)
                if s:
                    chains[stream, way, s - 1].wait_recv()
                    value = value + rs_in[m, stream, way, s - 1].astype(F32)
                rs_out[m, stream, way, s] = value.astype(BF16)
                chains[stream, way, s] = copy(
                    rs_out.at[m, stream, way, s],
                    rs_in.at[m, stream, way, s],
                    above if way == 0 else below,
                )

        def end_z(stream):
            value = part(stream, 0)
            for way in range(2):
                last = hops[stream][way] - 1
                chains[stream, way, last].wait_recv()
                value = value + rs_in[m, stream, way, last].astype(F32)
            return value

        def begin():
            send_y(0)
            send_y(1)
            step_z(0, 0)
            step_z(1, 0)

        def rest_y():
            for k in range(2, 8):
                send_y(k)

        last_y = []

        def end_first():
            rs_last_out[m] = end_z(0).astype(BF16)
            last_y.append(copy(rs_last_out.at[m], rs_last_in.at[m], partner))

        def end_others():
            node_input[m, lower] = end_z(1)
            node_input[m, upper] = end_z(2)

        def end():
            arrive(last_y)
            node_input[m, lower] += rs_last_in[m].astype(F32)

        return begin, rest_y, step_z, end_first, end_others, end

    def run(work, count=1):
        for _ in range(count):
            next(work, None)

    def finish(work):
        for _ in work:
            pass

    def network(m):
        turned = jnp.transpose(
            jnp.concatenate([node_input[m], jnp.zeros((64, NODES), F32)], axis=0)
        )[:, :CHANNELS].astype(BF16)
        hidden[m] = silu(mm(turned, encoder[...]))
        yield
        for layer in range(LAYERS):
            normed = normalize(hidden[m])
            source_target[m, :NODES] = mm(normed, sender_w[layer]).astype(BF16)
            travelling = []
            for q in (2, 3, 0, 1):
                halo_out[m, layer, q] = mm(want_hot[q], source_target[m, :NODES]).astype(BF16)
                travelling.append(
                    copy(
                        halo_out.at[m, layer, q],
                        halo.at[m, layer, pl.ds((q ^ 1) * HCAP, HCAP)],
                        sides[q],
                    )
                )
            yield
            source_target[m, NODES:] = mm(normed, receiver_w[layer]).astype(BF16)
            for k in range(3):
                at = slice(k * 512, (k + 1) * 512)
                summed[m, at] = mm(edge_hot[at, : 2 * NODES], source_target[m])
                yield
            arrive(travelling)
            for k in range(3):
                at = slice(k * 512, (k + 1) * 512)
                value = summed[m, at] + mm(edge_hot[at, 2 * NODES :], halo[m, layer])
                message[m, at] = silu(value).astype(BF16)
                yield
            collected = mm(collect_hot[...], message[m]).astype(BF16)
            hidden[m] += mm(collected, update_w[layer])
            yield
        both[m, 0, 0] = nt_dot(decoder[...], normalize(hidden[m])).astype(BF16)

    lengths = ((3, 4), (4, 3), (4, 3))
    low_half, high_half = pl.ds(0, HALF), pl.ds(HALF, HALF)

    def slot_of(way, s):
        return s if way == 0 else (N_Z - s) % N_Z

    def gather_all(m):
        moves, y_moves = {}, {}

        def view(stream, slot):
            return both.at[m, stream % 2, slot, high_half if stream == 2 else low_half]

        def pass_y(slot):
            y_moves[slot] = copy(
                both.at[m, 0, slot, high_half], both.at[m, 1, slot, high_half], partner
            )

        def forward(stream, s):
            for way in range(2):
                if s and s <= lengths[stream][way]:
                    moves[stream, way, s - 1].wait_recv()
                    if stream == 2:
                        pass_y(slot_of(way, s))
                if s < lengths[stream][way]:
                    moves[stream, way, s] = copy(
                        view(stream, slot_of(way, s)),
                        view(stream, slot_of(way, s + 1)),
                        above if way == 0 else below,
                    )

        def add(side, slots):
            total = None
            for slot in slots:
                if side:
                    y_moves[slot].wait_recv()
                    k = (2 * slot + 2 * y + N_LON - 1) % N_LON
                else:
                    k = 2 * slot
                term = mm(both[m, side, slot], spread[k])
                total = term if total is None else total + term
            adjust[m] += total

        across = []

        def begin():
            across.append(copy(view(0, 0), view(1, 0), partner))
            forward(2, 0)
            forward(0, 0)
            pass_y(0)

        def begin_other():
            arrive(across)
            forward(1, 0)

        def end():
            for j in range(ROWS):
                tile[m, pl.ds(j, CHANNELS, stride=ROWS), :] = adjust[
                    m, :, j * COLS : (j + 1) * COLS
                ]
            done = pltpu.make_async_copy(tile.at[m], out_hbm.at[m], load_sem.at[7 + m])
            done.start()
            results.append(done)

        return begin, begin_other, forward, add, end

    results = []

    def wanted_table():
        arrive(wanted)
        for q in range(4):
            rows = column(want_in[q, (q ^ 1) : (q ^ 1) + 1, :])[:HCAP]
            for part_of in range(2):
                want_hot[q, :, part_of * 128 : part_of * 128 + 128] = hot(
                    rows == lanes((HCAP, 128)) + part_of * 128
                )
        for m in range(MEMBERS):
            for layer in range(LAYERS):
                halo[m, layer, 4 * HCAP :] = jnp.zeros((NODES - 4 * HCAP, HID), BF16)

    def spread_table(k, carry):
        rows = pack_in[k]
        spot = sublanes((NODES, ENTRIES)).astype(F32)
        weights, places = [], []
        for slot in range(CAP):
            weights.append(
                jnp.where(spot == rows[slot : slot + 1], rows[4 + slot : 5 + slot], 0.0).astype(BF16)
            )
        weighted = jnp.concatenate(weights, axis=1)
        for j in range(4):
            places = [
                hot(spot + j * NODES == rows[2 + slot : 3 + slot]) for slot in range(CAP)
            ]
            spread[k, :, j * NODES : (j + 1) * NODES] = nt_dot(
                weighted, jnp.concatenate(places, axis=1)
            ).astype(BF16)
        return carry

    arrive(packs)
    wanted_table()
    lax.fori_loop(0, 4, spread_table, 0)
    arrive(second[0])
    arrive(second[1])
    for m in range(MEMBERS):
        advance(state_b, state_a, 1, m, True)
    lax.fori_loop(0, BLOCKS // 2, gather, 0)
    sums = [reduce_scatter(m) for m in range(MEMBERS)]
    begin0, rest0, step0, first0, others0, end0 = sums[0]
    begin1, rest1, step1, first1, others1, end1 = sums[1]
    begin0()
    begin1()
    rest0()
    lax.fori_loop(4, 8, spread_table, 0)
    step0(2, 0)
    rest1()
    step0(0, 1)
    step0(1, 1)
    step1(0, 1)
    step1(1, 1)
    step1(2, 0)
    lax.fori_loop(8, 12, spread_table, 0)
    step0(2, 1)
    step0(0, 2)
    step0(1, 2)
    step1(0, 2)
    step1(1, 2)
    lax.fori_loop(12, 16, spread_table, 0)
    step0(2, 2)
    step0(0, 3)
    step0(1, 3)
    step1(2, 1)
    step1(0, 3)
    step1(1, 3)
    for name in ("encoder", "sender", "receiver", "update", "decoder"):
        loads[name].wait()
    step0(2, 3)
    first0()
    step1(2, 2)
    first1()
    others0()
    end0()
    nets = [network(m) for m in range(MEMBERS)]
    net0, net1 = nets
    start_a, other_a, pass_a, add_a, end_a = gather_all(0)
    start_b, other_b, pass_b, add_b, end_b = gather_all(1)
    run(net0, 2)
    step1(2, 3)
    run(net0, 3)
    others1()
    end1()
    run(net1, 2)
    run(net1, 3)
    run(net0)
    run(net0, 4)
    run(net1)
    run(net1, 4)
    run(net0, 3)
    run(net0)
    finish(net0)
    start_a()
    for m in range(MEMBERS):
        for j in range(ROWS):
            adjust[m, :, j * COLS : (j + 1) * COLS] = state_a[
                j, m * CHANNELS : (m + 1) * CHANNELS, :
            ]
    run(net1, 3)
    run(net1)
    finish(net1)
    start_b()
    other_a()
    pass_a(2, 1)
    pass_a(0, 1)
    add_a(0, [0])
    add_b(0, [0])
    other_b()
    pass_b(2, 1)
    pass_b(0, 1)
    pass_a(2, 2)
    pass_a(1, 1)
    pass_a(0, 2)
    add_a(1, [0])
    pass_b(2, 2)
    pass_b(1, 1)
    pass_b(0, 2)
    add_a(0, [1, 7])
    add_b(1, [0])
    pass_a(2, 3)
    pass_a(1, 2)
    pass_a(0, 3)
    add_a(1, [1, 7])
    add_b(0, [1, 7])
    pass_b(2, 3)
    pass_b(1, 2)
    pass_b(0, 3)
    add_b(1, [1, 7])
    add_a(0, [2, 6])
    pass_a(2, 4)
    pass_a(1, 3)
    pass_a(0, 4)
    add_a(1, [2, 6])
    add_a(0, [3, 5])
    add_a(0, [4])
    add_b(0, [2, 6])
    pass_b(2, 4)
    pass_b(1, 3)
    pass_b(0, 4)
    add_b(1, [2, 6])
    add_b(0, [3, 5])
    add_b(0, [4])
    pass_a(1, 4)
    add_a(1, [3, 5])
    add_a(1, [4])
    end_a()
    pass_b(1, 4)
    add_b(1, [3, 5])
    add_b(1, [4])
    end_b()
    for c in started:
        c.wait_send()
    for c in results:
        c.wait()


def body(
    fields,
    wind_east,
    wind_north,
    diffusion,
    inflow_owner,
    inflow_cell,
    inflow_node,
    inflow_weight,
    encoder,
    sender_weight,
    receiver_weight,
    update_weight,
    decoder,
    edge_sender,
    edge_receiver,
    halo_rows,
    outflow_owner,
    outflow_node,
    outflow_cell,
    outflow_weight,
):
    vmem = pl.BlockSpec(memory_space=pltpu.VMEM)
    smem = pl.BlockSpec(memory_space=pltpu.SMEM)
    anywhere = pl.BlockSpec(memory_space=pl.ANY)
    half = (HALF, NODES)
    scratch = [
        pltpu.VMEM((MEMBERS, CHANNELS * ROWS, COLS), F32),
        pltpu.VMEM((ROWS, FEATURES, COLS), F32),
        pltpu.VMEM((ROWS, FEATURES, COLS), F32),
        pltpu.VMEM((DSTEPS, MEMBERS, 2, CHANNELS, COLS), BF16),
        pltpu.VMEM((DSTEPS, MEMBERS, 2, CHANNELS, COLS), BF16),
        pltpu.VMEM((DSTEPS, MEMBERS, GROUP, COLS), BF16),
        pltpu.VMEM((DSTEPS, MEMBERS, 2, GROUP, COLS), BF16),
        pltpu.VMEM((FEATURES, CELLS), BF16),
        pltpu.VMEM((BLOCKS // 2, CELLS, 2 * ENTRIES), BF16),
        pltpu.VMEM((BLOCKS + 1, FEATURES, ENTRIES), BF16),
        pltpu.VMEM((BLOCKS + 1, NODES, ENTRIES), BF16),
        pltpu.VMEM((N_LON, 8, ENTRIES), F32),
        pltpu.VMEM((N_LON, 8, ENTRIES), F32),
        pltpu.VMEM((4, 8, 128), jnp.int32),
        pltpu.VMEM((N_LON, FEATURES, NODES), F32),
        pltpu.VMEM((MEMBERS, 3, 2, 4) + half, BF16),
        pltpu.VMEM((MEMBERS, 3, 2, 4) + half, BF16),
        pltpu.VMEM((MEMBERS, N_Z) + half, BF16),
        pltpu.VMEM((MEMBERS, N_Z) + half, BF16),
        pltpu.VMEM((MEMBERS,) + half, BF16),
        pltpu.VMEM((MEMBERS,) + half, BF16),
        pltpu.VMEM((MEMBERS, CHANNELS, NODES), F32),
        pltpu.VMEM((EDGES, 3 * NODES), BF16),
        pltpu.VMEM((NODES, EDGES), BF16),
        pltpu.VMEM((4, HCAP, NODES), BF16),
        pltpu.VMEM((CHANNELS, HID), BF16),
        pltpu.VMEM((LAYERS, HID, HID), BF16),
        pltpu.VMEM((LAYERS, HID, HID), BF16),
        pltpu.VMEM((LAYERS, HID, HID), BF16),
        pltpu.VMEM((CHANNELS, HID), BF16),
        pltpu.VMEM((MEMBERS, NODES, HID), F32),
        pltpu.VMEM((MEMBERS, 2 * NODES, HID), BF16),
        pltpu.VMEM((MEMBERS, LAYERS, 4, HCAP, HID), BF16),
        pltpu.VMEM((MEMBERS, LAYERS, NODES, HID), BF16),
        pltpu.VMEM((MEMBERS, EDGES, HID), F32),
        pltpu.VMEM((MEMBERS, EDGES, HID), BF16),
        pltpu.VMEM((N_LON, NODES, CELLS), BF16),
        pltpu.VMEM((MEMBERS, 2, N_Z, CHANNELS, NODES), BF16),
        pltpu.VMEM((MEMBERS, CHANNELS, CELLS), F32),
        pltpu.SMEM((N_LON * CAP,), jnp.int32),
        pltpu.VMEM((8, 128), jnp.int32),
        pltpu.SemaphoreType.DMA((9,)),
        pltpu.SemaphoreType.DMA((COPIES,)),
        pltpu.SemaphoreType.DMA((COPIES,)),
    ]
    result = pl.pallas_call(
        kernel,
        out_shape=jax.ShapeDtypeStruct((MEMBERS, CHANNELS * ROWS, COLS), F32),
        in_specs=[smem, smem, anywhere]
        + [vmem] * 6
        + [anywhere] * 5
        + [vmem] * 6,
        out_specs=anywhere,
        scratch_shapes=scratch,
        compiler_params=pltpu.CompilerParams(
            collective_id=0, has_side_effects=True, vmem_limit_bytes=VMEM_LIMIT
        ),
    )(
        inflow_owner.reshape(1, BLOCKS),
        outflow_owner.reshape(1, BLOCKS),
        fields.reshape(MEMBERS, CHANNELS * ROWS, COLS),
        wind_east,
        wind_north,
        diffusion,
        inflow_cell,
        inflow_node,
        inflow_weight,
        encoder,
        sender_weight,
        receiver_weight,
        update_weight,
        decoder.T,
        edge_sender,
        edge_receiver,
        halo_rows,
        outflow_node,
        outflow_cell,
        outflow_weight,
    )
    return result.reshape(MEMBERS, CHANNELS, ROWS, COLS)


def solution(mesh):
    placed = (
        P("member", None, "lat", "lon"),
        P("lat", "lon"),
        P("lat", "lon"),
        P("lat", "lon"),
        P(("lat", "lon"), None),
        P(("lat", "lon"), None),
        P(("lat", "lon"), None),
        P(("lat", "lon"), None),
        P(),
        P(),
        P(),
        P(),
        P(),
        P("lat", "lon", None),
        P("lat", "lon", None),
        P("lat", "lon", None, None),
        P(("lat", "lon"), None),
        P(("lat", "lon"), None),
        P(("lat", "lon"), None),
        P(("lat", "lon"), None),
    )
    return jax.shard_map(
        body, mesh=mesh, in_specs=placed, out_specs=P("member", None, "lat", "lon"), check_vma=False
    )
```

time: 123 us -> 104 us (0.85)
  Pallas kernels: 113 us -> 101 us
  other arithmetic: 5.49 us -> 0 us
  local copies, waits for them, and re-layouts: 3.93 us -> 2.65 us
    pallas_call x1, Pallas kernels: 113 us -> 101 us  [body(): pl.pallas_call(kernel, out_shape=jax.ShapeDtypeStruct((MEMBERS, CHANNELS...]
    unnamed x2 -> x0, other arithmetic: 2.61 us -> none
    pad x1 -> x0, local copies, waits for them, and re-layouts: 1.28 us -> none  [body(): wanted = jnp.pad(halo_rows.reshape(4, HCAP), ((0, 4), (0, 128 - HCAP)))]
    reduce_min x2 -> x0, other arithmetic: 1.28 us -> none  [blocks_of(): jnp.min(jnp.where(hits, jnp.arange(BLOCKS, dtype=jnp.int32)[None, :], BLO...]
where the time goes in v2:
time: 104 us
  Pallas kernels  101 us (97%)
  local copies, waits for them, and re-layouts  2.65 us (3%)
    pallas_call x1, Pallas kernels, body(): pl.pallas_call(kernel, out_shape=jax.ShapeDtypeStruct((MEMBERS, CHANNELS...  101 us
    unnamed x1, local copies, waits for them, and re-layouts  2.65 us

profile of v2, /device:TPU:2, one launch (start us, length us, event | category | flops | bytes accessed | tf_op | source)
XLA Modules:
  0.0 103.8 jit_solution(5371959795028593131)
XLA Ops:
  0.0 101.2 %shard_map.190 = f32[2,1536,128]{2,1,0:T(8,128)} custom-call(s32[1,16]{1,0:T(1,128)} %bitcast.8, s32[1,16]{1,0:T(1,128)} %bitcast.9, f32[2,1536,128]{2,1,0:T(8,128)} %bitcast.6, f32[8,128]{1,0:T(8,128)} %wind_east.1, f32[8,128]{1,0:T(8,128)} %wind_north.1, f32[8,128]{1,0:T(8,128)} %diffusion.1, s32[16,128]{1,0:T(8,128)} %inflow_cell.1, ...), custom_call_target="tpu_custom_call" | custom-call | tf_op jit(solution)/shard_map/pallas_call | solution.py:767
  101.2 2.7 %copy.22 = f32[2,192,8,128]{3,2,1,0:T(8,128)} copy(f32[2,192,8,128]{3,2,1,0:T(8,128)} %bitcast.5) | data formatting | bytes 3145728

commit v3 on v2

--- a/solution.py
+++ b/solution.py
@@ -23,7 +23,7 @@
 N_Z = N_LON // 2
 GROUP = 48
 GROUPS = CHANNELS // GROUP
-HALF = CHANNELS // 2
+HALF = 80
 COPIES = 192
 VMEM_LIMIT = 63 * 1024 * 1024
 
@@ -360,6 +360,7 @@
     order = (4, -3, 3, -2, 2, -1, 1, 0)
     hops = ((4, 3), (3, 4), (4, 3))
     lower, upper = slice(0, HALF), slice(HALF, CHANNELS)
+    widths = (HALF, HALF, CHANNELS - HALF)
 
     def reduce_scatter(m):
         y_copies, chains = {}, {}
@@ -384,11 +385,12 @@
                 value = part(stream, dz)
                 if s:
                     chains[stream, way, s - 1].wait_recv()
-                    value = value + rs_in[m, stream, way, s - 1].astype(F32)
-                rs_out[m, stream, way, s] = value.astype(BF16)
+                    value = value + rs_in[m, stream, way, s - 1, : widths[stream]].astype(F32)
+                width = widths[stream]
+                rs_out[m, stream, way, s, :width] = value.astype(BF16)
                 chains[stream, way, s] = copy(
-                    rs_out.at[m, stream, way, s],
-                    rs_in.at[m, stream, way, s],
+                    rs_out.at[m, stream, way, s, pl.ds(0, width)],
+                    rs_in.at[m, stream, way, s, pl.ds(0, width)],
                     above if way == 0 else below,
                 )
 
@@ -397,7 +399,7 @@
             for way in range(2):
                 last = hops[stream][way] - 1
                 chains[stream, way, last].wait_recv()
-                value = value + rs_in[m, stream, way, last].astype(F32)
+                value = value + rs_in[m, stream, way, last, : widths[stream]].astype(F32)
             return value
 
         def begin():
@@ -471,7 +473,7 @@
         both[m, 0, 0] = nt_dot(decoder[...], normalize(hidden[m])).astype(BF16)
 
     lengths = ((3, 4), (4, 3), (4, 3))
-    low_half, high_half = pl.ds(0, HALF), pl.ds(HALF, HALF)
+    low_half, high_half = pl.ds(0, HALF), pl.ds(HALF, CHANNELS - HALF)
 
     def slot_of(way, s):
         return s if way == 0 else (N_Z - s) % N_Z
@@ -570,9 +572,8 @@
     arrive(packs)
     wanted_table()
     lax.fori_loop(0, 4, spread_table, 0)
-    arrive(second[0])
-    arrive(second[1])
     for m in range(MEMBERS):
+        arrive(second[m])
         advance(state_b, state_a, 1, m, True)
     lax.fori_loop(0, BLOCKS // 2, gather, 0)
     sums = [reduce_scatter(m) for m in range(MEMBERS)]
@@ -717,7 +718,7 @@
     vmem = pl.BlockSpec(memory_space=pltpu.VMEM)
     smem = pl.BlockSpec(memory_space=pltpu.SMEM)
     anywhere = pl.BlockSpec(memory_space=pl.ANY)
-    half = (HALF, NODES)
+    half = (CHANNELS - HALF, NODES)
     scratch = [
         pltpu.VMEM((MEMBERS, CHANNELS * ROWS, COLS), F32),
         pltpu.VMEM((ROWS, FEATURES, COLS), F32),
@@ -738,8 +739,8 @@
         pltpu.VMEM((MEMBERS, 3, 2, 4) + half, BF16),
         pltpu.VMEM((MEMBERS, N_Z) + half, BF16),
         pltpu.VMEM((MEMBERS, N_Z) + half, BF16),
-        pltpu.VMEM((MEMBERS,) + half, BF16),
-        pltpu.VMEM((MEMBERS,) + half, BF16),
+        pltpu.VMEM((MEMBERS, HALF, NODES), BF16),
+        pltpu.VMEM((MEMBERS, HALF, NODES), BF16),
         pltpu.VMEM((MEMBERS, CHANNELS, NODES), F32),
         pltpu.VMEM((EDGES, 3 * NODES), BF16),
         pltpu.VMEM((NODES, EDGES), BF16),

time: 104 us -> 102 us (0.981)
  Pallas kernels: 101 us -> 98.8 us
    pallas_call x1, Pallas kernels: 101 us -> 98.8 us  [body(): pl.pallas_call(kernel, out_shape=jax.ShapeDtypeStruct((MEMBERS, CHANNELS...]
where the time goes in v3:
time: 102 us; the launch traced here: 101 us
  Pallas kernels  98.8 us (97%)
  local copies, waits for them, and re-layouts  2.65 us (3%)
    pallas_call x1, Pallas kernels, body(): pl.pallas_call(kernel, out_shape=jax.ShapeDtypeStruct((MEMBERS, CHANNELS...  98.8 us
    unnamed x1, local copies, waits for them, and re-layouts  2.65 us

profile of v3, /device:TPU:2, one launch (start us, length us, event | category | flops | bytes accessed | tf_op | source)
XLA Modules:
  0.0 101.4 jit_solution(15735953366411579591)
XLA Ops:
  0.0 98.8 %shard_map.190 = f32[2,1536,128]{2,1,0:T(8,128)} custom-call(s32[1,16]{1,0:T(1,128)} %bitcast.8, s32[1,16]{1,0:T(1,128)} %bitcast.9, f32[2,1536,128]{2,1,0:T(8,128)} %bitcast.6, f32[8,128]{1,0:T(8,128)} %wind_east.1, f32[8,128]{1,0:T(8,128)} %wind_north.1, f32[8,128]{1,0:T(8,128)} %diffusion.1, s32[16,128]{1,0:T(8,128)} %inflow_cell.1, ...), custom_call_target="tpu_custom_call" | custom-call | tf_op jit(solution)/shard_map/pallas_call | solution.py:768
  98.8 2.7 %copy.22 = f32[2,192,8,128]{3,2,1,0:T(8,128)} copy(f32[2,192,8,128]{3,2,1,0:T(8,128)} %bitcast.5) | data formatting | bytes 3145728

commit v4 on v3

--- a/solution.py
+++ b/solution.py
@@ -239,7 +239,7 @@
                 carry = jnp.where(lane // 2 == 8 * g + j, moved, carry)
             return carry
 
-        edge = lax.fori_loop(0, GROUPS, collect, jnp.zeros((GROUP, COLS), F32))
+        edge = lax.fori_loop(0, GROUPS, collect, jnp.zeros((GROUP, COLS), F32), unroll=2)
         lon_out[step, m] = edge.astype(BF16)
         return [
             copy(lon_out.at[step, m], lon_in.at[step, m, 1], sides[2]),
@@ -277,7 +277,7 @@
                     grid_bf[at, j * COLS : (j + 1) * COLS] = value.astype(BF16)
             return carry
 
-        lax.fori_loop(0, GROUPS, group, 0)
+        lax.fori_loop(0, GROUPS, group, 0, unroll=2)
 
     def arrive(copies):
         for c in copies:
@@ -575,7 +575,7 @@
     for m in range(MEMBERS):
         arrive(second[m])
         advance(state_b, state_a, 1, m, True)
-    lax.fori_loop(0, BLOCKS // 2, gather, 0)
+    lax.fori_loop(0, BLOCKS // 2, gather, 0, unroll=4)
     sums = [reduce_scatter(m) for m in range(MEMBERS)]
     begin0, rest0, step0, first0, others0, end0 = sums[0]
     begin1, rest1, step1, first1, others1, end1 = sums[1]

time: 102 us -> 99.5 us (0.975)
  Pallas kernels: 98.8 us -> 96.7 us
    pallas_call x1, Pallas kernels: 98.8 us -> 96.7 us  [body(): pl.pallas_call(kernel, out_shape=jax.ShapeDtypeStruct((MEMBERS, CHANNELS...]
where the time goes in v4:
time: 99.5 us; the launch traced here: 99.4 us
  Pallas kernels  96.7 us (97%)
  local copies, waits for them, and re-layouts  2.65 us (3%)
    pallas_call x1, Pallas kernels, body(): pl.pallas_call(kernel, out_shape=jax.ShapeDtypeStruct((MEMBERS, CHANNELS...  96.7 us
    unnamed x1, local copies, waits for them, and re-layouts  2.65 us

profile of v4, /device:TPU:2, one launch (start us, length us, event | category | flops | bytes accessed | tf_op | source)
XLA Modules:
  0.0 99.4 jit_solution(17457161431044782985)
XLA Ops:
  0.0 96.7 %shard_map.190 = f32[2,1536,128]{2,1,0:T(8,128)} custom-call(s32[1,16]{1,0:T(1,128)} %bitcast.8, s32[1,16]{1,0:T(1,128)} %bitcast.9, f32[2,1536,128]{2,1,0:T(8,128)} %bitcast.6, f32[8,128]{1,0:T(8,128)} %wind_east.1, f32[8,128]{1,0:T(8,128)} %wind_north.1, f32[8,128]{1,0:T(8,128)} %diffusion.1, s32[16,128]{1,0:T(8,128)} %inflow_cell.1, ...), custom_call_target="tpu_custom_call" | custom-call | tf_op jit(solution)/shard_map/pallas_call | solution.py:768
  96.7 2.7 %copy.22 = f32[2,192,8,128]{3,2,1,0:T(8,128)} copy(f32[2,192,8,128]{3,2,1,0:T(8,128)} %bitcast.5) | data formatting | bytes 3145728
